TPU v7x, 8 devices: a whole 2x2x1 slice. The times are simulated.
8 devices in a mesh: dp: 1 (over z), sp: 8 (over y, x, core).
Axes of the slice: x: 2, y: 2, z: 1, core: 2. Of those that a mesh axis runs over, the one named last changes fastest.
Arguments:
- hidden: bfloat16 [1024, 2560], P(('dp', 'sp'))
- ln_gain: bfloat16 [2560], replicated
- w_q: bfloat16 [2560, 4096], replicated
- w_k: bfloat16 [2560, 1024], replicated
- w_v: bfloat16 [2560, 1024], replicated
- w_o: bfloat16 [4096, 2560], replicated
- q_gain: bfloat16 [128], replicated
- k_gain: bfloat16 [128], replicated
Outputs:
- output: bfloat16 [1024, 2560], P(('dp', 'sp'))
All inputs are finite; a program needn't handle non-finite values.
Results may differ from a plain program's by a relative error of at most 0.00712467.
Values are sent between devices in bfloat16 or wider.
A program may use at most 1 GiB of HBM per device.

v0:
```python
import jax
import jax.numpy as jnp
from jax import lax
from jax.sharding import PartitionSpec as P

EPS = 1e-6
THETA = 1000000.0


def head_norm(values, gain):
    return values * lax.rsqrt(jnp.mean(values * values, axis=-1, keepdims=True) + EPS) * gain.astype(jnp.float32)


def rotate(values, positions):
    head_dim = values.shape[-1]
    half = head_dim // 2
    inv_freq = jnp.power(THETA, -(jnp.arange(half, dtype=jnp.float32) * (2.0 / head_dim)))
    angles = positions.astype(jnp.float32)[:, None] * inv_freq[None, :]
    cos_pos = jnp.cos(angles)[:, None, :]
    sin_pos = jnp.sin(angles)[:, None, :]
    first_half = values[..., :half]
    second_half = values[..., half:]
    return jnp.concatenate([first_half * cos_pos - second_half * sin_pos, second_half * cos_pos + first_half * sin_pos], axis=-1)


def project(hidden, ln_gain, w_q, w_k, w_v, q_gain, k_gain, positions):
    tokens = hidden.shape[0]
    head_dim = q_gain.shape[0]
    hidden_f32 = hidden.astype(jnp.float32)
    normed = (hidden_f32 * lax.rsqrt(jnp.mean(hidden_f32 * hidden_f32, axis=-1, keepdims=True) + EPS) * ln_gain.astype(jnp.float32)).astype(jnp.bfloat16)
    q_raw = jnp.dot(normed, w_q, preferred_element_type=jnp.float32).reshape(tokens, -1, head_dim)
    k_raw = jnp.dot(normed, w_k, preferred_element_type=jnp.float32).reshape(tokens, -1, head_dim)
    v_local = jnp.dot(normed, w_v, preferred_element_type=jnp.float32).astype(jnp.bfloat16).reshape(tokens, -1, head_dim)
    q_local = rotate(head_norm(q_raw, q_gain), positions).astype(jnp.bfloat16)
    k_local = rotate(head_norm(k_raw, k_gain), positions).astype(jnp.bfloat16)
    return hidden_f32, q_local, k_local, v_local


def attend(q_all, k_all, v_all, q_start):
    q_rows, q_heads, head_dim = q_all.shape
    k_rows = k_all.shape[0]
    k_heads = k_all.shape[1]
    group = q_heads // k_heads
    limit = 2 ** 25 // (q_heads * k_rows)
    block_rows = min(q_rows, 2 ** max(3, min(9, limit.bit_length() - 1)))
    num_blocks = q_rows // block_rows
    q_blocks = q_all.reshape(num_blocks, block_rows, k_heads, group, head_dim)
    key_pos = jnp.arange(k_rows)
    score_scale = head_dim ** -0.5

    def one_block(block_args):
        q_block, block_idx = block_args
        scores = jnp.einsum('qkgd,skd->kgqs', q_block, k_all, preferred_element_type=jnp.float32) * score_scale
        q_pos = q_start + block_idx * block_rows + jnp.arange(block_rows)
        visible = q_pos[:, None] >= key_pos[None, :]
        scores = jnp.where(visible, scores, -jnp.inf)
        attn_prob = jax.nn.softmax(scores, axis=-1).astype(jnp.bfloat16)
        mixed = jnp.einsum('kgqs,skd->qkgd', attn_prob, v_all, preferred_element_type=jnp.float32)
        return mixed.astype(jnp.bfloat16)

    outputs = lax.map(one_block, (q_blocks, jnp.arange(num_blocks)))
    return outputs.reshape(q_rows, q_heads, head_dim)


def finish(hidden_f32, mixed, w_o):
    tokens = mixed.shape[0]
    result = hidden_f32 + jnp.dot(mixed.reshape(tokens, -1), w_o, preferred_element_type=jnp.float32)
    return result.astype(jnp.bfloat16)


def solution(mesh):
    group_size = mesh.shape['sp']

    def device_step(hidden, ln_gain, w_q, w_k, w_v, w_o, q_gain, k_gain):
        tokens = hidden.shape[0]
        head_dim = q_gain.shape[0]
        kv_heads = w_k.shape[1] // head_dim
        copies = max(1, group_size // kv_heads)
        positions = lax.axis_index('sp') * tokens + jnp.arange(tokens)
        hidden_f32, q_local, k_local, v_local = project(hidden, ln_gain, w_q, w_k, w_v, q_gain, k_gain, positions)
        q_heads = lax.all_to_all(q_local, 'sp', 1, 0, tiled=True)
        k_heads = lax.all_to_all(jnp.repeat(k_local, copies, axis=1), 'sp', 1, 0, tiled=True)
        v_heads = lax.all_to_all(jnp.repeat(v_local, copies, axis=1), 'sp', 1, 0, tiled=True)
        mixed = attend(q_heads, k_heads, v_heads, 0)
        mixed_local = lax.all_to_all(mixed, 'sp', 0, 1, tiled=True)
        return finish(hidden_f32, mixed_local, w_o)

    row_spec = P(('dp', 'sp'), None)
    return jax.shard_map(device_step, mesh=mesh, in_specs=(row_spec, P(), P(), P(), P(), P(), P(), P()), out_specs=row_spec, check_vma=False)
```

profile of v0, /device:TPU:0, one launch (start us, length us, event | category | flops | bytes accessed | tf_op | source)
XLA Modules:
  0.0 101.8 jit_solution(2448643498235840425)
XLA Ops:
  0.0 0.7 convert_element_type.47
  0.7 1.3 %fusion.25 = f32[128]{0:T(128)S(1)} fusion(bf16[128,2560]{1,0:T(8,128)(2,1)} %param.10), kind=kLoop, calls=%fused_computation.30 | loop fusion | flops 982912 | bytes 655872 | tf_op jit(solution)/shard_map/reduce_sum | solution.py:30
  2.0 3.6 %fusion.31 = f32[128,1024]{1,0:T(8,128)S(1)} fusion(bf16[2560,1024]{1,0:T(8,128)(2,1)} %param.13, bf16[128,2560]{1,0:T(8,128)(2,1)} %param.10, f32[2560]{0:T(1024)S(1)} %convert_element_type.47, f32[128]{0:T(128)S(1)} %add_rsqrt_fusion.2), kind=kOutput, calls=%fused_computation.50 | convolution fusion | flops 672399360 | bytes 6433280 | tf_op jit(solution)/shard_map/dot_general | solution.py:32
  6.8 0.9 pad_maximum_fusion.1
  7.7 4.3 %all-to-all-start.1 = ((bf16[128,8,128]{2,0,1:T(8,128)(2,1)}), bf16[128,8,128]{2,0,1:T(8,128)(2,1)S(1)}, u32[]{:S(2)}, u32[]{:S(2)}) async-start(bf16[128,8,128]{2,0,1:T(8,128)(2,1)} %pad_maximum_fusion.1), calls=%async_computation.1 | async-start | bytes 524288 | tf_op jit(solution)/shard_map/all_to_all | solution.py:82
  12.0 8.6 %fusion.33 = f32[128,4096]{1,0:T(8,128)S(1)} fusion(bf16[2560,4096]{1,0:T(8,128)(2,1)} %param.12, bf16[128,2560]{1,0:T(8,128)(2,1)S(1)} %copy-done, f32[2560]{0:T(1024)S(1)} %convert_element_type.47, f32[128]{0:T(128)S(1)} %add_rsqrt_fusion.2), kind=kOutput, calls=%fused_computation.51 | convolution fusion | flops 2685665280 | bytes 23734784 | tf_op jit(solution)/shard_map/dot_general | solution.py:31
  20.6 0.4 copy.69
  21.0 0.6 multiply_reduce_fusion
  21.7 0.7 fusion.24
  22.4 0.8 subtract_convert_fusion
  23.2 1.6 %pad_maximum_fusion = bf16[128,32,128]{2,0,1:T(8,128)(2,1)} fusion(bf16[128,32,64]{2,0,1:T(8,128)(2,1)S(1)} %get-tuple-element.108, bf16[128,32,64]{2,0,1:T(8,128)(2,1)S(1)} %get-tuple-element.107), kind=kLoop, calls=%fused_computation.35 | loop fusion | flops 2097152 | bytes 2097152 | tf_op jit(solution)/shard_map/concatenate | solution.py:23
  24.8 2.9 %all-to-all-start = ((bf16[128,32,128]{2,0,1:T(8,128)(2,1)}), bf16[128,32,128]{2,0,1:T(8,128)(2,1)S(1)}, u32[]{:S(2)}, u32[]{:S(2)}) async-start(bf16[128,32,128]{2,0,1:T(8,128)(2,1)} %pad_maximum_fusion), calls=%async_computation | async-start | bytes 2097152 | tf_op jit(solution)/shard_map/all_to_all | solution.py:81
  27.7 3.4 %fusion.28 = bf16[16,8,8,128]{3,2,1,0:T(8,128)(2,1)S(1)} fusion(bf16[2560,1024]{1,0:T(8,128)(2,1)} %param.14, bf16[128,2560]{1,0:T(8,128)(2,1)S(1)} %copy-done, f32[2560]{0:T(1024)S(1)} %convert_element_type.47, f32[128]{0:T(128)S(1)} %add_rsqrt_fusion.2), kind=kOutput, calls=%fused_computation.34 | convolution fusion | flops 672530432 | bytes 6171136 | tf_op jit(solution)/shard_map/dot_general | solution.py:33
  31.1 0.8 copy.74
  31.8 11.2 %all-to-all-done = bf16[128,32,128]{2,0,1:T(8,128)(2,1)S(1)} async-done(((bf16[128,32,128]{2,0,1:T(8,128)(2,1)}), bf16[128,32,128]{2,0,1:T(8,128)(2,1)S(1)}, u32[]{:S(2)}, u32[]{:S(2)}) %all-to-all-start) | async-done | bytes 1048608 | tf_op jit(solution)/shard_map/all_to_all | solution.py:81
  43.0 2.3 %all-to-all-start.2 = ((bf16[128,8,128]{2,0,1:T(8,128)(2,1)}), bf16[128,8,128]{2,0,1:T(8,128)(2,1)S(1)}, u32[]{:S(2)}, u32[]{:S(2)}) async-start(bf16[128,8,128]{2,0,1:T(8,128)(2,1)} %bitcast.106), calls=%async_computation.2 | async-start | bytes 524288 | tf_op jit(solution)/shard_map/all_to_all | solution.py:83
  45.5 6.3 %all-to-all-done.2 = bf16[128,8,128]{2,0,1:T(8,128)(2,1)S(1)} async-done(((bf16[128,8,128]{2,0,1:T(8,128)(2,1)}), bf16[128,8,128]{2,0,1:T(8,128)(2,1)S(1)}, u32[]{:S(2)}, u32[]{:S(2)}) %all-to-all-start.2) | async-done | bytes 262176 | tf_op jit(solution)/shard_map/all_to_all | solution.py:83
  51.8 19.8 %while.11 = (s32[]{:T(128)}, bf16[2,512,1,4,128]{4,1,0,3,2:T(8,128)(2,1)}, s32[2]{0:T(128)S(1)}, bf16[2,512,1,4,128]{4,1,0,3,2:T(8,128)(2,1)S(1)}, bf16[1024,1,1...) while((s32[]{:T(128)}, ...), condition=%wide.region_6.7_spmd.clone, body=%wide.region_3.6_spmd.clone.sunk | while | flops 1099690496 | bytes 37269680 | solution.py:61
  51.8 0.6 dynamic_slice.19
  53.4 1.7 %fusion.49 = (f32[4,512]{1,0:T(4,128)S(1)}, f32[512,4,1024]{2,0,1:T(8,128)S(1)}) fusion(pred[512,1024]{1,0:T(8,128)(4,1)S(1)} %iota_compare_fusion.2, bf16[1024,1,128]{2,0,1:T(8,128)(2,1)S(1)} %get-tuple-element.174, bf16[2,512,1,4,128]{4,1,0,3,2:T(8,128)(2,1)S(1)} %get-tuple-element.173, s32[]{:T(128)} %get-tuple-element.162), kind=kOutput, calls=%fused_computation.5.clone.1 | convolution fusion | flops 543160320 | bytes 9707524 | tf_op jit(solution)/shard_map/while/body/eval_jaxpr/qkgd,skd->kgqs/dot_general | solution.py:53
  55.1 2.4 %fusion.50 = f32[4,512]{1,0:T(4,128)S(1)} fusion(f32[512,4,1024]{2,0,1:T(8,128)S(1)} %get-tuple-element.152, f32[4,512]{1,0:T(4,128)S(1)} %get-tuple-element.153, pred[512,1024]{1,0:T(8,128)(4,1)S(1)} %iota_compare_fusion.2), kind=kLoop, calls=%fused_computation.4.clone.1 | loop fusion | flops 8386560 | bytes 8929280 | tf_op jit(solution)/shard_map/while/body/eval_jaxpr/reduce_sum | solution.py:57
  57.6 3.2 %fusion.51 = bf16[2,512,1,4,128]{4,1,0,3,2:T(8,128)(2,1)S(1)} fusion(bf16[2,512,1,4,128]{4,1,0,3,2:T(8,128)(2,1)S(1)} %copy-done.1, s32[]{:T(128)} %get-tuple-element.162, f32[4,512]{1,0:T(4,128)S(1)} %fusion.50, f32[4,512]{1,0:T(4,128)S(1)} %get-tuple-element.153, f32[512,4,1024]{2,0,1:T(8,128)S(1)} %get-tuple-element.152, ...), kind=kOutput, calls=%fused_computation.11.clone.1 | convolution fusion | flops 547618816 | bytes 9715716 | tf_op jit(solution)/shard_map/while/body/eval_jaxpr/kgqs,skd->qkgd/dot_general | solution.py:58
  60.8 1.0 copy-done.2
  61.7 0.6 dynamic_slice.19
  63.4 1.7 %fusion.49 = (f32[4,512]{1,0:T(4,128)S(1)}, f32[512,4,1024]{2,0,1:T(8,128)S(1)}) fusion(pred[512,1024]{1,0:T(8,128)(4,1)S(1)} %iota_compare_fusion.2, bf16[1024,1,128]{2,0,1:T(8,128)(2,1)S(1)} %get-tuple-element.174, bf16[2,512,1,4,128]{4,1,0,3,2:T(8,128)(2,1)S(1)} %get-tuple-element.173, s32[]{:T(128)} %get-tuple-element.162), kind=kOutput, calls=%fused_computation.5.clone.1 | convolution fusion | flops 543160320 | bytes 9707524 | tf_op jit(solution)/shard_map/while/body/eval_jaxpr/qkgd,skd->kgqs/dot_general | solution.py:53
  65.1 2.4 %fusion.50 = f32[4,512]{1,0:T(4,128)S(1)} fusion(f32[512,4,1024]{2,0,1:T(8,128)S(1)} %get-tuple-element.152, f32[4,512]{1,0:T(4,128)S(1)} %get-tuple-element.153, pred[512,1024]{1,0:T(8,128)(4,1)S(1)} %iota_compare_fusion.2), kind=kLoop, calls=%fused_computation.4.clone.1 | loop fusion | flops 8386560 | bytes 8929280 | tf_op jit(solution)/shard_map/while/body/eval_jaxpr/reduce_sum | solution.py:57
  67.5 3.2 %fusion.51 = bf16[2,512,1,4,128]{4,1,0,3,2:T(8,128)(2,1)S(1)} fusion(bf16[2,512,1,4,128]{4,1,0,3,2:T(8,128)(2,1)S(1)} %copy-done.1, s32[]{:T(128)} %get-tuple-element.162, f32[4,512]{1,0:T(4,128)S(1)} %fusion.50, f32[4,512]{1,0:T(4,128)S(1)} %get-tuple-element.153, f32[512,4,1024]{2,0,1:T(8,128)S(1)} %get-tuple-element.152, ...), kind=kOutput, calls=%fused_computation.11.clone.1 | convolution fusion | flops 547618816 | bytes 9715716 | tf_op jit(solution)/shard_map/while/body/eval_jaxpr/kgqs,skd->qkgd/dot_general | solution.py:58
  70.7 1.0 copy-done.2
  71.7 2.0 %copy.60 = bf16[1024,4,128]{2,1,0:T(4,128)(2,1)S(1)} copy(bf16[1024,4,128]{2,0,1:T(8,128)(2,1)} %bitcast.134) | data formatting | bytes 2097152 | tf_op jit(solution)/shard_map/reshape | solution.py:62
  73.7 16.5 %all_to_all.66 = bf16[1024,4,128]{2,1,0:T(4,128)(2,1)S(1)} all-to-all(bf16[1024,4,128]{2,1,0:T(4,128)(2,1)S(1)} %copy.60), channel_id=1, replica_groups=mesh['dp'=1,'sp'=8] {'sp'}, dimensions={0} | all-to-all | bytes 2097152 | tf_op jit(solution)/shard_map/all_to_all | solution.py:85
  90.4 0.7 copy.62
  91.0 10.7 %fusion.23 = bf16[128,2560]{1,0:T(8,128)(2,1)} fusion(bf16[128,4096]{0,1:T(8,128)(2,1)S(1)} %bitcast.129, bf16[4096,2560]{1,0:T(8,128)(2,1)} %param.15, bf16[128,2560]{1,0:T(8,128)(2,1)S(1)} %copy-done), kind=kOutput, calls=%fused_computation.22 | convolution fusion | flops 2685337600 | bytes 23330816 | tf_op jit(solution)/shard_map/dot_general | solution.py:67
  (35 shorter events, 2.2 us)
Async XLA Ops:
  2.0 4.0 %copy-start.3 = (bf16[128]{0:T(256)(128)(2,1)S(1)}, bf16[128]{0:T(256)(128)(2,1)}, u32[]{:S(2)}) copy-start(bf16[128]{0:T(256)(128)(2,1)} %param.17) | copy-start | bytes 772
  6.0 6.0 %copy-start = (bf16[128,2560]{1,0:T(8,128)(2,1)S(1)}, bf16[128,2560]{1,0:T(8,128)(2,1)}, u32[]{:S(2)}) copy-start(bf16[128,2560]{1,0:T(8,128)(2,1)} %param.10) | copy-start | bytes 1966084
  7.7 17.1 %all-to-all-start.1 = ((bf16[128,8,128]{2,0,1:T(8,128)(2,1)}), bf16[128,8,128]{2,0,1:T(8,128)(2,1)S(1)}, u32[]{:S(2)}, u32[]{:S(2)}) async-start(bf16[128,8,128]{2,0,1:T(8,128)(2,1)} %pad_maximum_fusion.1), calls=%async_computation.1 | async-start | bytes 524288 | tf_op jit(solution)/shard_map/all_to_all | solution.py:82
  20.9 0.7 copy-start.4
  24.8 18.3 %all-to-all-start = ((bf16[128,32,128]{2,0,1:T(8,128)(2,1)}), bf16[128,32,128]{2,0,1:T(8,128)(2,1)S(1)}, u32[]{:S(2)}, u32[]{:S(2)}) async-start(bf16[128,32,128]{2,0,1:T(8,128)(2,1)} %pad_maximum_fusion), calls=%async_computation | async-start | bytes 2097152 | tf_op jit(solution)/shard_map/all_to_all | solution.py:81
  43.0 8.8 %all-to-all-start.2 = ((bf16[128,8,128]{2,0,1:T(8,128)(2,1)}), bf16[128,8,128]{2,0,1:T(8,128)(2,1)S(1)}, u32[]{:S(2)}, u32[]{:S(2)}) async-start(bf16[128,8,128]{2,0,1:T(8,128)(2,1)} %bitcast.106), calls=%async_computation.2 | async-start | bytes 524288 | tf_op jit(solution)/shard_map/all_to_all | solution.py:83
  55.1 2.4 %copy-start.1 = (bf16[2,512,1,4,128]{4,1,0,3,2:T(8,128)(2,1)S(1)}, bf16[2,512,1,4,128]{4,1,0,3,2:T(8,128)(2,1)}, u32[]{:S(2)}) copy-start(bf16[2,512,1,4,128]{4,1,0,3,2:T(8,128)(2,1)} %get-tuple-element.163) | copy-start | bytes 3145732 | tf_op jit(solution)/shard_map/while
  60.8 1.0 copy-start.2
  65.1 2.4 %copy-start.1 = (bf16[2,512,1,4,128]{4,1,0,3,2:T(8,128)(2,1)S(1)}, bf16[2,512,1,4,128]{4,1,0,3,2:T(8,128)(2,1)}, u32[]{:S(2)}) copy-start(bf16[2,512,1,4,128]{4,1,0,3,2:T(8,128)(2,1)} %get-tuple-element.163) | copy-start | bytes 3145732 | tf_op jit(solution)/shard_map/while
  70.7 1.0 copy-start.2
where the time goes:
time: 102 us
  matrix products  36 us (35%)
  waiting for transfers between devices  17.5 us (17%)
  blocking collectives  16.5 us (16%)
  other arithmetic  13.1 us (13%)
  starting transfers between devices  9.55 us (9%)
  local copies, waits for them, and re-layouts  7.38 us (7%)
  loops' own time  1.4 us (1%)
    all_to_all x1, blocking collectives, device_step(): mixed_local = lax.all_to_all(mixed, 'sp', 0, 1, tiled=True)  16.5 us
    all_to_all x1, waiting for transfers between devices, device_step(): q_heads = lax.all_to_all(q_local, 'sp', 1, 0, tiled=True)  11.2 us
    dot_general x1, matrix products, finish(): jnp.dot(mixed.reshape(tokens, -1), w_o, preferred_element_type=jnp.float32)  10.7 us
    dot_general x1, matrix products, project(): jnp.dot(normed, w_q, preferred_element_type=jnp.float32)  8.57 us
    dot_general x2, matrix products, one_block(): jnp.einsum('kgqs,skd->qkgd', attn_prob, v_all, preferred_element_type=jnp...  6.37 us
    all_to_all x1, waiting for transfers between devices, device_step(): lax.all_to_all(jnp.repeat(v_local, copies, axis=1), 'sp', 1, 0, tiled=True)  6.33 us
    reduce_sum x2, other arithmetic, one_block(): attn_prob = jax.nn.softmax(scores, axis=-1).astype(jnp.bfloat16)  4.85 us
    all_to_all x1, starting transfers between devices, device_step(): lax.all_to_all(jnp.repeat(k_local, copies, axis=1), 'sp', 1, 0, tiled=True)  4.31 us
  transfers between devices with their start and end apart: 3, of which 2 were waited for; matrix products, arithmetic and copies ran while one was open for 17% of the time, Pallas kernels for 0%

commit v1 on v0

v1 whole, which is shorter than its diff:
```python
import functools

import jax
import jax.numpy as jnp
import numpy as np
from jax import lax
from jax.experimental import pallas as pl
from jax.experimental.pallas import tpu as pltpu
from jax.sharding import PartitionSpec as P

EPS = 1e-6
THETA = 1000000.0
MESH = pl.DeviceIdType.MESH
F32 = jnp.float32
BF16 = jnp.bfloat16
LANES = 128
LOG2E = 1.4426950408889634


def rope_table(seq, head_dim):
    half = head_dim // 2
    inv_freq = np.power(np.float32(THETA), -(np.arange(half, dtype=np.float32) * np.float32(2.0 / head_dim))).astype(np.float32)
    angles = (np.arange(seq, dtype=np.float32)[:, None] * inv_freq[None, :]).astype(np.float32).astype(np.float64)
    return np.concatenate([np.cos(angles), np.sin(angles)], axis=1).astype(np.float32)


def kernel(x_hbm, ln_gain, w_q, w_k, w_v, w_o, q_gain, k_gain, tab_hbm, out_hbm,
           x_v, h_v, tab_v, wk_v, wv_v, wq_v, wo_v, kbuf, vbuf, qbuf, m_s, acc_s, res, out_v,
           in_sem, wk_sem, wv_sem, wq_sem, wo_sem, out_sem,
           own_sem, fwd_sem, relay_sem, krecv, vrecv):
    rows, d = x_v.shape
    n_kv, seq, hd = kbuf.shape
    group = qbuf.shape[1] // rows
    n_pairs = wk_v.shape[0]
    chips = seq // (2 * rows)
    block = 2 * rows
    me = lax.axis_index("sp")
    core = lax.rem(me, 2)
    chip = me // 2
    sibling = me + 1 - 2 * core
    score_scale = hd ** -0.5 * LOG2E

    x_copy = pltpu.make_async_copy(x_hbm, x_v, in_sem.at[0])
    tab_copy = pltpu.make_async_copy(tab_hbm.at[pl.ds(pl.multiple_of(me * rows, rows), rows)], tab_v, in_sem.at[1])
    x_copy.start()

    def wk_copy(p):
        return pltpu.make_async_copy(w_k.at[:, pl.ds(pl.multiple_of(p * 2 * hd, 2 * hd), 2 * hd)], wk_v.at[p], wk_sem.at[p])

    def wv_copy(p):
        return pltpu.make_async_copy(w_v.at[:, pl.ds(pl.multiple_of(p * 2 * hd, 2 * hd), 2 * hd)], wv_v.at[p], wv_sem.at[p])

    def wq_copy(h):
        n = group * hd
        return pltpu.make_async_copy(w_q.at[:, pl.ds(pl.multiple_of(h * n, n), n)], wq_v.at[h], wq_sem.at[h])

    def wo_copy(h):
        n = group * hd
        return pltpu.make_async_copy(w_o.at[pl.ds(pl.multiple_of(h * n, n), n)], wo_v.at[h], wo_sem.at[h])

    wk_copy(0).start()
    wv_copy(0).start()
    tab_copy.start()
    for p in range(1, n_pairs):
        wk_copy(p).start()
        wv_copy(p).start()
    for h in range(n_kv):
        wq_copy(h).start()
        wo_copy(h).start()

    barrier = pltpu.get_barrier_semaphore()
    pl.semaphore_signal(barrier, inc=1, device_id={"sp": sibling}, device_id_type=MESH)
    for step in range(1, chips):
        pl.semaphore_signal(barrier, inc=1, device_id={"sp": lax.rem(me + 2 * step, 2 * chips)}, device_id_type=MESH)

    def send(buf, h, src, dst, sem):
        part = buf.at[h, pl.ds(pl.multiple_of(src * rows, rows), rows)]
        recv = krecv if buf is kbuf else vrecv
        return pltpu.make_async_remote_copy(src_ref=part, dst_ref=part, send_sem=sem, recv_sem=recv.at[h, src],
                                            device_id={"sp": dst}, device_id_type=MESH)

    def arrived(buf, h, src):
        send(buf, h, src, sibling, fwd_sem.at[0, 0, 0]).wait_recv()

    x_copy.wait()
    xf = x_v[...].astype(F32)
    res[...] = xf
    norm = lax.rsqrt(jnp.mean(xf * xf, axis=-1, keepdims=True) + EPS)
    h_v[...] = (xf * norm * ln_gain[...].astype(F32)).astype(BF16)
    tab_copy.wait()
    table = tab_v[...]
    turned = pltpu.roll(table, hd // 2, 1)
    low = lax.broadcasted_iota(jnp.int32, table.shape, 1) < hd // 2
    cos_pos = jnp.where(low, table, turned)
    sin_pos = jnp.where(low, -turned, table)

    def head_norm_rotate(values, gain):
        gain = jnp.broadcast_to(gain[...].astype(F32), (8, hd))
        gain_turned = pltpu.roll(gain, hd // 2, 1)
        values = values * lax.rsqrt(jnp.mean(values * values, axis=-1, keepdims=True) + EPS)
        return (values * (cos_pos * gain[:1]) + pltpu.roll(values, hd // 2, 1) * (sin_pos * gain_turned[:1])).astype(BF16)

    my_rows = pl.ds(pl.multiple_of(me * rows, rows), rows)
    pl.semaphore_wait(barrier, chips)

    def send_own_far(h):
        send(vbuf, h, me, me + 2, own_sem.at[1, 1, h]).start()
        send(kbuf, h, me, me + 2, own_sem.at[0, 1, h]).start()

    def kv_pair(p, carry):
        wk_copy(p).wait()
        wv_copy(p).wait()
        keys = jnp.dot(h_v[...], wk_v[p], preferred_element_type=F32)
        vals = jnp.dot(h_v[...], wv_v[p], preferred_element_type=F32)
        for j in range(2):
            h = 2 * p + j
            cols = slice(j * hd, (j + 1) * hd)
            vbuf[h, my_rows, :] = vals[:, cols].astype(BF16)
            kbuf[h, my_rows, :] = head_norm_rotate(keys[:, cols], k_gain)
        for j in range(2):
            h = 2 * p + j
            send(kbuf, h, me, sibling, own_sem.at[0, 0, h]).start()
            send(vbuf, h, me, sibling, own_sem.at[1, 0, h]).start()

            @pl.when(chip == 0)
            def _():
                send(kbuf, h, me, me + 6, own_sem.at[0, 3, h]).start()
                send(vbuf, h, me, me + 2, own_sem.at[1, 1, h]).start()
                send(kbuf, h, me, me + 2, own_sem.at[0, 1, h]).start()
                send(vbuf, h, me, me + 4, own_sem.at[1, 2, h]).start()
                send(kbuf, h, me, me + 4, own_sem.at[0, 2, h]).start()

            @pl.when(chip == 1)
            def _():
                send(vbuf, h, me, me + 4, own_sem.at[1, 2, h]).start()
                send(kbuf, h, me, me + 4, own_sem.at[0, 2, h]).start()
                send(kbuf, h, me, me + 2, own_sem.at[0, 1, h]).start()

            @pl.when((chip == 2) & (p == 0))
            def _():
                send_own_far(h)
        return carry

    lax.fori_loop(0, n_pairs, kv_pair, 0)

    def project_q(h):
        wq_copy(h).wait()
        q = jnp.dot(h_v[...], wq_v[h], preferred_element_type=F32)
        for g in range(group):
            qbuf[h, g * rows:(g + 1) * rows, :] = head_norm_rotate(q[:, g * hd:(g + 1) * hd], q_gain)

    def relay(h):
        @pl.when(chip >= 2)
        def _():
            src = 2 * (chip - 2) + core
            arrived(vbuf, h, src)
            send(vbuf, h, src, 2 * (5 - chip) + core, relay_sem.at[h]).start()
            send(vbuf, h, src, sibling, fwd_sem.at[1, chip - 2, h]).start()

    def forward(buf, t, sc, h):
        src = 2 * sc + core
        arrived(buf, h, src)
        send(buf, h, src, sibling, fwd_sem.at[t, sc, h]).start()

    def direct(h):
        @pl.when(chip == 1)
        def _():
            forward(vbuf, 1, 0, h)
            forward(kbuf, 0, 0, h)

        @pl.when(chip == 2)
        def _():
            forward(kbuf, 0, 0, h)
            forward(vbuf, 1, 1, h)
            forward(kbuf, 0, 1, h)

        @pl.when(chip == 3)
        def _():
            forward(vbuf, 1, 2, h)
            forward(kbuf, 0, 2, h)
            forward(kbuf, 0, 1, h)
            forward(kbuf, 0, 0, h)
            forward(vbuf, 1, 0, h)

    ones = jnp.ones((block, hd), BF16)
    row_id = lax.broadcasted_iota(jnp.int32, (rows, block), 0)
    key_id = lax.broadcasted_iota(jnp.int32, (rows, block), 1)

    def scores_of(h, keys):
        return lax.dot_general(qbuf[h], kbuf[h, keys, :], (((1,), (1,)), ((), ())), preferred_element_type=F32)

    def weighted(probs, h, keys):
        return jnp.dot(probs, jnp.concatenate([vbuf[h, keys, :], ones], axis=1), preferred_element_type=F32)

    def attend_own(h):
        arrived(kbuf, h, sibling)
        arrived(vbuf, h, sibling)
        keys = pl.ds(pl.multiple_of(chip * block, block), block)
        scores = scores_of(h, keys)
        visible = key_id <= row_id + core * rows
        scores = jnp.where(jnp.concatenate([visible] * group, axis=0), scores, -jnp.inf)
        top = jnp.max(scores, axis=-1, keepdims=True)
        probs = jnp.exp2((scores - top) * score_scale).astype(BF16)
        m_s[...] = jnp.broadcast_to(top, m_s.shape)
        acc_s[...] = weighted(probs, h, keys)

    def attend_block(h, sc):
        arrived(kbuf, h, 2 * sc + 1 - core)
        arrived(vbuf, h, 2 * sc + 1 - core)
        keys = pl.ds(pl.multiple_of(sc * block, block), block)
        scores = scores_of(h, keys)
        old = m_s[...]
        top = jnp.maximum(old, jnp.max(scores, axis=-1, keepdims=True))
        top2 = jnp.concatenate([top, top], axis=1)
        probs = jnp.exp2((scores - top2) * score_scale).astype(BF16)
        decay = jnp.exp2((old - top) * score_scale)
        m_s[...] = top
        acc_s[...] = acc_s[...] * jnp.concatenate([decay, decay], axis=1) + weighted(probs, h, keys)

    def project_out(h):
        wo_copy(h).wait()
        mixed = (acc_s[:, :hd] / acc_s[:, hd:]).astype(BF16)
        mixed = jnp.concatenate([mixed[g * rows:(g + 1) * rows] for g in range(group)], axis=1)
        res[...] += jnp.dot(mixed, wo_v[h], preferred_element_type=F32)

    project_q(0)
    relay(0)
    project_q(1)
    relay(1)
    direct(0)
    attend_own(0)

    def head_step(h, carry):
        for sc in range(chips - 1):
            @pl.when(chip > sc)
            def _():
                attend_block(h, sc)

        @pl.when(h < n_kv - 2)
        def _():
            relay(h + 2)

            @pl.when(chip == 2)
            def _():
                send_own_far(h + 2)

        @pl.when(h < n_kv - 1)
        def _():
            direct(h + 1)

        project_out(h)

        @pl.when(h < n_kv - 2)
        def _():
            project_q(h + 2)

        @pl.when(h < n_kv - 1)
        def _():
            attend_own(h + 1)
        return carry

    lax.fori_loop(0, n_kv, head_step, 0)
    out_v[...] = res[...].astype(BF16)
    out_copy = pltpu.make_async_copy(out_v, out_hbm, out_sem)
    out_copy.start()

    def finish_sends(h, carry):
        def done(buf, src, sem):
            send(buf, h, src, sibling, sem).wait_send()

        done(kbuf, me, own_sem.at[0, 0, h])
        done(vbuf, me, own_sem.at[1, 0, h])

        @pl.when(chip <= 2)
        def _():
            done(kbuf, me, own_sem.at[0, 1, h])

        @pl.when((chip == 0) | (chip == 2))
        def _():
            done(vbuf, me, own_sem.at[1, 1, h])

        @pl.when(chip <= 1)
        def _():
            done(kbuf, me, own_sem.at[0, 2, h])
            done(vbuf, me, own_sem.at[1, 2, h])

        @pl.when(chip == 0)
        def _():
            done(kbuf, me, own_sem.at[0, 3, h])

        @pl.when(chip >= 2)
        def _():
            done(vbuf, 2 * (chip - 2) + core, relay_sem.at[h])
        for sc in range(chips - 1):
            @pl.when(chip > sc)
            def _():
                done(kbuf, 2 * sc + core, fwd_sem.at[0, sc, h])
                done(vbuf, 2 * sc + core, fwd_sem.at[1, sc, h])
        return carry

    lax.fori_loop(0, n_kv, finish_sends, 0)
    out_copy.wait()


def solution(mesh):
    def device_step(hidden, ln_gain, w_q, w_k, w_v, w_o, q_gain, k_gain):
        rows, d = hidden.shape
        hd = q_gain.shape[0]
        n_kv = w_k.shape[1] // hd
        group = w_q.shape[1] // w_k.shape[1]
        seq = rows * mesh.shape['sp']
        table = jnp.asarray(rope_table(seq, hd))
        any_spec = pl.BlockSpec(memory_space=pl.ANY)
        vmem_spec = pl.BlockSpec(memory_space=pltpu.VMEM)
        dma = pltpu.SemaphoreType.DMA
        return pl.pallas_call(
            kernel,
            out_shape=jax.ShapeDtypeStruct((rows, d), BF16),
            in_specs=[any_spec, vmem_spec, any_spec, any_spec, any_spec, any_spec, vmem_spec, vmem_spec, any_spec],
            out_specs=any_spec,
            scratch_shapes=[
                pltpu.VMEM((rows, d), BF16),
                pltpu.VMEM((rows, d), BF16),
                pltpu.VMEM((rows, hd), F32),
                pltpu.VMEM((n_kv // 2, d, 2 * hd), BF16),
                pltpu.VMEM((n_kv // 2, d, 2 * hd), BF16),
                pltpu.VMEM((n_kv, d, group * hd), BF16),
                pltpu.VMEM((n_kv, group * hd, d), BF16),
                pltpu.VMEM((n_kv, seq, hd), BF16),
                pltpu.VMEM((n_kv, seq, hd), BF16),
                pltpu.VMEM((n_kv, group * rows, hd), BF16),
                pltpu.VMEM((group * rows, LANES), F32),
                pltpu.VMEM((group * rows, 2 * hd), F32),
                pltpu.VMEM((rows, d), F32),
                pltpu.VMEM((rows, d), BF16),
                dma((2,)),
                dma((n_kv // 2,)),
                dma((n_kv // 2,)),
                dma((n_kv,)),
                dma((n_kv,)),
                dma,
                dma((2, 4, n_kv)),
                dma((2, 3, n_kv)),
                dma((n_kv,)),
                dma((n_kv, 8)),
                dma((n_kv, 8)),
            ],
            compiler_params=pltpu.CompilerParams(collective_id=0, has_side_effects=True, vmem_limit_bytes=67043328),
        )(hidden, ln_gain.reshape(1, -1), w_q, w_k, w_v, w_o, q_gain.reshape(1, -1), k_gain.reshape(1, -1), table)

    row_spec = P(('dp', 'sp'), None)
    return jax.shard_map(device_step, mesh=mesh, in_specs=(row_spec, P(), P(), P(), P(), P(), P(), P()), out_specs=row_spec, check_vma=False)
```

time: 102 us -> 56.2 us (0.55)
  the two profiles are of different devices: /device:TPU:0 before, /device:TPU:7 now
where the time goes in v1:
time: 56.2 us; the launch traced here: 55.9 us
  Pallas kernels  52.7 us (94%)
  local copies, waits for them, and re-layouts  3.26 us (6%)
    pallas_call x1, Pallas kernels, device_step(): pl.pallas_call(kernel, out_shape=jax.ShapeDtypeStruct((rows, d), BF16), i...  52.7 us
    unnamed x1, local copies, waits for them, and re-layouts  1.97 us
    reshape x1, local copies, waits for them, and re-layouts, device_step(): ln_gain.reshape(1, -1)  1.3 us

profile of v1, /device:TPU:7, one launch (start us, length us, event | category | flops | bytes accessed | tf_op | source)
XLA Modules:
  0.0 55.9 jit_solution(11581219185174315623)
XLA Ops:
  0.0 1.3 %reshape.9.ln_gain = bf16[1,2560]{1,0:T(2,128)(2,1)} reshape(bf16[2560]{0:T(1024)(128)(2,1)} %param.10) | data formatting | bytes 10240 | tf_op jit(solution)/shard_map/reshape | solution.py:349
  1.3 52.7 %shard_map.91 = bf16[128,2560]{1,0:T(8,128)(2,1)} custom-call(bf16[128,2560]{1,0:T(8,128)(2,1)} %x_hbm.1, bf16[1,2560]{1,0:T(2,128)(2,1)} %reshape.9.ln_gain, bf16[2560,4096]{1,0:T(8,128)(2,1)} %w_q.1, bf16[2560,1024]{1,0:T(8,128)(2,1)} %w_k.1, bf16[2560,1024]{1,0:T(8,128)(2,1)} %w_v.1, bf16[4096,2560]{1,0:T(8,128)(2,1)} %w_o.1, bf16[1,128]{1,0:T(2,128)(2,1)} %bitcast.2, ...), custom_call_target="tpu_custom_call" | custom-call | tf_op jit(solution)/shard_map/pallas_call | solution.py:316
  54.0 2.0 %copy.11 = bf16[128,2560]{1,0:T(8,128)(2,1)} copy(bf16[128,2560]{1,0:T(8,128)(2,1)} %shard_map.91) | data formatting | bytes 1310720

commit v2 on v0

v2 whole, which is shorter than its diff:
```python
import functools

import jax
import jax.numpy as jnp
import numpy as np
from jax import lax
from jax.experimental import pallas as pl
from jax.experimental.pallas import tpu as pltpu
from jax.sharding import PartitionSpec as P

EPS = 1e-6
THETA = 1000000.0
MESH = pl.DeviceIdType.MESH
F32 = jnp.float32
BF16 = jnp.bfloat16
LANES = 128
LOG2E = 1.4426950408889634
AHEAD = 2


def rope_table(seq, head_dim):
    half = head_dim // 2
    inv_freq = np.power(np.float32(THETA), -(np.arange(half, dtype=np.float32) * np.float32(2.0 / head_dim))).astype(np.float32)
    angles = (np.arange(seq, dtype=np.float32)[:, None] * inv_freq[None, :]).astype(np.float32).astype(np.float64)
    return np.concatenate([np.cos(angles), np.sin(angles)], axis=1).astype(np.float32)


def kernel(x_hbm, ln_gain_hbm, w_q, w_k, w_v, w_o, q_gain_hbm, k_gain_hbm, tab_hbm, out_v,
           x_v, h_v, ln_gain, q_gain, k_gain, tab_v, wk_v, wv_v, wq_v, wo_v, kbuf, vbuf, qraw, qbuf, mixed_t, res,
           in_sem, wk_sem, wv_sem, wq_sem, wo_sem,
           swap_send, swap_recv, far_sem, far_recv, fwd_send, relay_sem):
    rows, d = x_v.shape
    n_kv, n_dev, _, hd = kbuf.shape
    group = qbuf.shape[1] // rows
    n_pairs = wk_v.shape[0]
    wq_slots, wo_slots = wq_v.shape[0], wo_v.shape[0]
    chips = n_dev // 2
    me = lax.axis_index("sp")
    core = lax.rem(me, 2)
    chip = me // 2
    sibling = me + 1 - 2 * core
    score_scale = hd ** -0.5 * LOG2E

    x_copy = pltpu.make_async_copy(x_hbm, x_v, in_sem.at[0])
    small_copies = [
        pltpu.make_async_copy(ln_gain_hbm, ln_gain, in_sem.at[1]),
        pltpu.make_async_copy(q_gain_hbm, q_gain, in_sem.at[2]),
        pltpu.make_async_copy(k_gain_hbm, k_gain, in_sem.at[3]),
        pltpu.make_async_copy(tab_hbm.at[pl.ds(pl.multiple_of(me * rows, rows), rows)], tab_v, in_sem.at[4]),
    ]

    def wk_copy(p):
        return pltpu.make_async_copy(w_k.at[:, pl.ds(pl.multiple_of(p * 2 * hd, 2 * hd), 2 * hd)], wk_v.at[p], wk_sem.at[lax.rem(p, 2)])

    def wv_copy(p):
        return pltpu.make_async_copy(w_v.at[:, pl.ds(pl.multiple_of(p * 2 * hd, 2 * hd), 2 * hd)], wv_v.at[p], wv_sem.at[lax.rem(p, 2)])

    def wq_copy(h):
        n = group * hd
        slot = lax.rem(h, wq_slots)
        return pltpu.make_async_copy(w_q.at[:, pl.ds(pl.multiple_of(h * n, n), n)], wq_v.at[slot], wq_sem.at[slot])

    def wo_copy(h):
        n = group * hd
        slot = lax.rem(h, wo_slots)
        return pltpu.make_async_copy(w_o.at[pl.ds(pl.multiple_of(h * n, n), n)], wo_v.at[slot], wo_sem.at[slot])

    x_copy.start()
    for copy in small_copies:
        copy.start()
    wk_copy(0).start()
    wv_copy(0).start()

    barrier = pltpu.get_barrier_semaphore()
    for step in range(1, n_dev):
        pl.semaphore_signal(barrier, inc=1, device_id={"sp": lax.rem(me + step, n_dev)}, device_id_type=MESH)

    def swap(buf, t, h):
        part = buf.at[h, me]
        return pltpu.make_async_remote_copy(src_ref=part, dst_ref=part, send_sem=swap_send.at[t], recv_sem=swap_recv.at[t, h],
                                            device_id={"sp": sibling}, device_id_type=MESH)

    def swapped(buf, t, h):
        part = buf.at[h, sibling]
        pltpu.make_async_remote_copy(src_ref=part, dst_ref=part, send_sem=swap_send.at[t], recv_sem=swap_recv.at[t, h],
                                     device_id={"sp": sibling}, device_id_type=MESH).wait_recv()

    def send(buf, h, sc, dst, sem):
        part = buf.at[h, pl.ds(2 * sc, 2)]
        t = 0 if buf is kbuf else 1
        return pltpu.make_async_remote_copy(src_ref=part, dst_ref=part, send_sem=sem, recv_sem=far_recv.at[t, h, sc],
                                            device_id={"sp": dst}, device_id_type=MESH)

    def arrived(buf, h, sc):
        send(buf, h, sc, sibling, fwd_send.at[0]).wait_recv()

    with jax.named_scope("gain_wait"):
        small_copies[0].wait()
    gain_rows = ln_gain[...].astype(F32)

    with jax.named_scope("x_wait"):
        x_copy.wait()
    wk_copy(1).start()
    wv_copy(1).start()
    for r in range(0, rows, 16):
        xf = x_v[r:r + 16, :].astype(F32)
        norm = lax.rsqrt(jnp.mean(xf * xf, axis=-1, keepdims=True) + EPS)
        for c in range(d // LANES):
            cols = slice(c * LANES, (c + 1) * LANES)
            h_v[r:r + 16, cols] = (xf[:, cols] * norm * gain_rows[c:c + 1, :]).astype(BF16)

    with jax.named_scope("small_wait"):
        for copy in small_copies[1:]:
            copy.wait()
    table = tab_v[...]
    turned = pltpu.roll(table, hd // 2, 1)
    low = lax.broadcasted_iota(jnp.int32, table.shape, 1) < hd // 2
    cos_pos = jnp.where(low, table, turned)
    sin_pos = jnp.where(low, -turned, table)

    def head_norm_rotate(values, gain):
        gain = jnp.broadcast_to(gain[...].astype(F32), (8, hd))
        gain_turned = pltpu.roll(gain, hd // 2, 1)
        values = values * lax.rsqrt(jnp.mean(values * values, axis=-1, keepdims=True) + EPS)
        return (values * (cos_pos * gain[:1]) + pltpu.roll(values, hd // 2, 1) * (sin_pos * gain_turned[:1])).astype(BF16)

    with jax.named_scope("barrier"):
        pl.semaphore_wait(barrier, n_dev - 1)

    def far_send(h):
        @pl.when((chip == 0) & (core == 1))
        def _():
            send(vbuf, h, 0, 3, far_sem.at[0]).start()
            send(kbuf, h, 0, 6, far_sem.at[1]).start()
            send(kbuf, h, 0, 2, far_sem.at[2]).start()

        @pl.when((chip == 0) & (core == 0))
        def _():
            send(vbuf, h, 0, 5, far_sem.at[0]).start()
            send(kbuf, h, 0, 4, far_sem.at[1]).start()

        @pl.when((chip == 1) & (core == 0))
        def _():
            send(vbuf, h, 1, 7, far_sem.at[0]).start()
            send(kbuf, h, 1, 6, far_sem.at[1]).start()

        @pl.when((chip == 1) & (core == 1))
        def _():
            send(kbuf, h, 1, 4, far_sem.at[1]).start()

        @pl.when((chip == 2) & (core == 1))
        def _():
            send(vbuf, h, 2, 7, far_sem.at[0]).start()
            send(kbuf, h, 2, 6, far_sem.at[1]).start()

    def swap_in(p):
        with jax.named_scope("swap_in"):
            for j in range(2):
                swapped(kbuf, 0, 2 * p + j)
                swapped(vbuf, 1, 2 * p + j)

        @pl.when(p < AHEAD // 2)
        def _():
            far_send(2 * p)
            far_send(2 * p + 1)

    def kv_pair(p, carry):
        with jax.named_scope("wkv_wait"):
            wk_copy(p).wait()
            wv_copy(p).wait()

        @pl.when(p < n_pairs - 2)
        def _():
            wk_copy(p + 2).start()
            wv_copy(p + 2).start()

        @pl.when(p >= n_pairs - 2)
        def _():
            wq_copy(p - (n_pairs - 2)).start()

        keys = jnp.dot(h_v[...], wk_v[p], preferred_element_type=F32)
        vals = jnp.dot(h_v[...], wv_v[p], preferred_element_type=F32)
        for j in range(2):
            h = 2 * p + j
            cols = slice(j * hd, (j + 1) * hd)
            kbuf[h, me] = head_norm_rotate(keys[:, cols], k_gain)
            vbuf[h, me] = vals[:, cols].T.astype(BF16)
        for j in range(2):
            swap(kbuf, 0, 2 * p + j).start()
            swap(vbuf, 1, 2 * p + j).start()

        @pl.when(p > 0)
        def _():
            swap_in(p - 1)
        return carry

    lax.fori_loop(0, n_pairs, kv_pair, 0)

    def q_dot(h):
        qraw[lax.rem(h, 2)] = jnp.dot(h_v[...], wq_v[lax.rem(h, wq_slots)], preferred_element_type=F32)

    def q_finish(h):
        q = qraw[lax.rem(h, 2)]
        for g in range(group):
            qbuf[h, g * rows:(g + 1) * rows, :] = head_norm_rotate(q[:, g * hd:(g + 1) * hd], q_gain)

    def wq_wait(h):
        with jax.named_scope("wq_wait"):
            wq_copy(h).wait()

    @jax.named_scope("relay")
    def relay(h):
        @pl.when((chip >= 2) & (core == 1))
        def _():
            sc = chip - 2
            arrived(vbuf, h, sc)
            send(vbuf, h, sc, 11 - 2 * chip, relay_sem).start()
            send(vbuf, h, sc, sibling, fwd_send.at[sc]).start()

    def forward(buf, h, sc):
        arrived(buf, h, sc)
        send(buf, h, sc, sibling, fwd_send.at[sc]).start()

    @jax.named_scope("direct")
    def direct(h):
        @pl.when((chip >= 1) & (core == 0))
        def _():
            for sc in range(chips - 2, -1, -1):
                @pl.when(chip > sc)
                def _():
                    forward(kbuf, h, sc)

        @pl.when((chip >= 1) & (core == 1))
        def _():
            for sc in range(chips - 2, -1, -1):
                @pl.when((chip > sc) & (chip != sc + 2))
                def _():
                    forward(vbuf, h, sc)

    def attend(h, c):
        if c:
            with jax.named_scope("block_wait"):
                for sc in range(c - 1, -1, -1):
                    @pl.when(core == 0)
                    def _():
                        arrived(vbuf, h, sc)

                    @pl.when(core == 1)
                    def _():
                        arrived(kbuf, h, sc)
        n_keys = 2 * (c + 1) * rows
        keys = kbuf[h, 0:2 * (c + 1)].reshape(n_keys, hd)
        scores = lax.dot_general(keys, qbuf[h], (((1,), (1,)), ((), ())), preferred_element_type=F32)
        key_id = lax.broadcasted_iota(jnp.int32, (2 * rows, rows), 0)
        row_id = lax.broadcasted_iota(jnp.int32, (2 * rows, rows), 1)
        visible = jnp.concatenate([key_id <= row_id + core * rows] * group, axis=1)
        last = jnp.where(visible, scores[n_keys - 2 * rows:], -jnp.inf)
        scores = jnp.concatenate([scores[:n_keys - 2 * rows], last], axis=0) if c else last
        top = jnp.max(scores, axis=0, keepdims=True)
        probs = jnp.exp2((scores - top) * score_scale)
        total = jnp.sum(probs, axis=0, keepdims=True)
        vals = jnp.concatenate([vbuf[h, src] for src in range(2 * (c + 1))], axis=1)
        mixed = jnp.dot(vals, probs.astype(BF16), preferred_element_type=F32)
        mixed_t[...] = (mixed / total).astype(BF16)

    def out_dot():
        mixed = jnp.concatenate([mixed_t[:, g * rows:(g + 1) * rows].T for g in range(group)], axis=1)
        return mixed

    def project_out(h, mixed):
        res[...] += jnp.dot(mixed, wo_v[lax.rem(h, wo_slots)], preferred_element_type=F32)

    wq_copy(2).start()
    wo_copy(0).start()
    swap_in(n_pairs - 1)
    wq_wait(0)
    q_dot(0)
    relay(0)
    wq_copy(3).start()
    wo_copy(1).start()
    wq_wait(1)
    with jax.named_scope("q_first"):
        q_finish(0)
        q_dot(1)
    relay(1)
    direct(0)
    for r in range(0, rows, 16):
        res[r:r + 16, :] = x_v[r:r + 16, :].astype(F32)

    def head_step(h, carry):
        for c in range(chips):
            @pl.when(chip == c)
            @jax.named_scope("attend")
            def _():
                attend(h, c)

        @pl.when(h < n_kv - 2)
        def _():
            relay(h + 2)

        @pl.when(h < n_kv - AHEAD)
        def _():
            far_send(h + AHEAD)

        @pl.when(h < n_kv - 1)
        def _():
            direct(h + 1)

        with jax.named_scope("wo_wait"):
            wo_copy(h).wait()

        @pl.when(h < n_kv - 2)
        def _():
            wo_copy(h + 2).start()
            wq_wait(h + 2)

        @pl.when(h < n_kv - 4)
        def _():
            wq_copy(h + 4).start()

        @pl.when(h < n_kv - 2)
        @jax.named_scope("project")
        def _():
            q_finish(h + 1)
            mixed = out_dot()
            project_out(h, mixed)
            q_dot(h + 2)

        @pl.when(h >= n_kv - 2)
        @jax.named_scope("project_end")
        def _():
            @pl.when(h == n_kv - 2)
            def _():
                q_finish(h + 1)
            project_out(h, out_dot())
        return carry

    lax.fori_loop(0, n_kv, head_step, 0)
    out_v[...] = res[...].astype(BF16)

    def finish(buf, sc, sem):
        part = buf.at[:, pl.ds(2 * sc, 2)]
        pltpu.make_async_remote_copy(src_ref=part, dst_ref=part, send_sem=sem, recv_sem=far_recv.at[0, 0, 0],
                                     device_id={"sp": sibling}, device_id_type=MESH).wait_send()

    with jax.named_scope("finish_sends"):
        for t, buf in enumerate((kbuf, vbuf)):
            part = buf.at[:, me]
            pltpu.make_async_remote_copy(src_ref=part, dst_ref=part, send_sem=swap_send.at[t], recv_sem=far_recv.at[0, 0, 0],
                                         device_id={"sp": sibling}, device_id_type=MESH).wait_send()

        @pl.when((chip == 0) | ((chip + core == 1) | (chip + core == 3)) & (chip < 3))
        def _():
            finish(vbuf, 0, far_sem.at[0])

        @pl.when((chip < 2) | ((chip == 2) & (core == 1)))
        def _():
            finish(kbuf, 0, far_sem.at[1])

        @pl.when((chip == 0) & (core == 1))
        def _():
            finish(kbuf, 0, far_sem.at[2])

        @pl.when((chip >= 2) & (core == 1))
        def _():
            finish(vbuf, 0, relay_sem)
        for sc in range(chips - 1):
            @pl.when(chip > sc)
            def _():
                finish(kbuf, sc, fwd_send.at[sc])


def write_back(res_v, out_hbm, sem):
    copy = pltpu.make_async_copy(res_v, out_hbm, sem)
    copy.start()
    copy.wait()


def solution(mesh):
    def device_step(hidden, ln_gain, w_q, w_k, w_v, w_o, q_gain, k_gain):
        rows, d = hidden.shape
        hd = q_gain.shape[0]
        n_kv = w_k.shape[1] // hd
        group = w_q.shape[1] // w_k.shape[1]
        n_dev = mesh.shape['sp']
        table = jnp.asarray(rope_table(rows * n_dev, hd))
        any_spec = pl.BlockSpec(memory_space=pl.ANY)
        vmem_spec = pl.BlockSpec(memory_space=pltpu.VMEM)
        dma = pltpu.SemaphoreType.DMA
        result = pl.pallas_call(
            kernel,
            out_shape=pltpu.VMEM((rows, d), BF16),
            in_specs=[any_spec] * 9,
            out_specs=vmem_spec,
            scratch_shapes=[
                pltpu.VMEM((rows, d), BF16),
                pltpu.VMEM((rows, d), BF16),
                pltpu.VMEM((d // LANES, LANES), BF16),
                pltpu.VMEM((1, hd), BF16),
                pltpu.VMEM((1, hd), BF16),
                pltpu.VMEM((rows, hd), F32),
                pltpu.VMEM((n_kv // 2, d, 2 * hd), BF16),
                pltpu.VMEM((n_kv // 2, d, 2 * hd), BF16),
                pltpu.VMEM((5, d, group * hd), BF16),
                pltpu.VMEM((4, group * hd, d), BF16),
                pltpu.VMEM((n_kv, n_dev, rows, hd), BF16),
                pltpu.VMEM((n_kv, n_dev, hd, rows), BF16),
                pltpu.VMEM((2, rows, group * hd), F32),
                pltpu.VMEM((n_kv, group * rows, hd), BF16),
                pltpu.VMEM((hd, group * rows), BF16),
                pltpu.VMEM((rows, d), F32),
                dma((5,)),
                dma((2,)),
                dma((2,)),
                dma((5,)),
                dma((4,)),
                dma((2,)),
                dma((2, n_kv)),
                dma((3,)),
                dma((2, n_kv, n_dev // 2 - 1)),
                dma((n_dev // 2 - 1,)),
                dma,
            ],
            compiler_params=pltpu.CompilerParams(collective_id=0, has_side_effects=True, vmem_limit_bytes=62000000),
        )(hidden, ln_gain.reshape(-1, LANES), w_q, w_k, w_v, w_o, q_gain.reshape(1, -1), k_gain.reshape(1, -1), table)
        return pl.pallas_call(
            write_back,
            out_shape=jax.ShapeDtypeStruct((rows, d), BF16),
            in_specs=[vmem_spec],
            out_specs=any_spec,
            scratch_shapes=[dma],
            compiler_params=pltpu.CompilerParams(vmem_limit_bytes=1000000),
        )(result)

    row_spec = P(('dp', 'sp'), None)
    return jax.shard_map(device_step, mesh=mesh, in_specs=(row_spec, P(), P(), P(), P(), P(), P(), P()), out_specs=row_spec, check_vma=False)
```

time: 102 us -> 33.7 us (0.33)
  the two profiles are of different devices: /device:TPU:0 before, /device:TPU:7 now
where the time goes in v2:
time: 33.7 us; the launch traced here: 33.6 us
  Pallas kernels  33.6 us (100%)
    pallas_call x1, Pallas kernels, device_step(): pl.pallas_call(kernel, out_shape=pltpu.VMEM((rows, d), BF16), in_specs=[a...  32.7 us
    pallas_call x1, Pallas kernels, device_step(): pl.pallas_call(write_back, out_shape=jax.ShapeDtypeStruct((rows, d), BF16...  0.85 us

profile of v2, /device:TPU:7, one launch (start us, length us, event | category | flops | bytes accessed | tf_op | source)
XLA Modules:
  0.0 33.6 jit_solution(6792410900390465187)
XLA Ops:
  0.0 32.7 %shard_map.91.res_v = bf16[128,2560]{1,0:T(8,128)(2,1)S(1)} custom-call(bf16[128,2560]{1,0:T(8,128)(2,1)} %x_hbm.1, bf16[20,128]{1,0:T(8,128)(2,1)} %bitcast.3, bf16[2560,4096]{1,0:T(8,128)(2,1)} %w_q.1, bf16[2560,1024]{1,0:T(8,128)(2,1)} %w_k.1, bf16[2560,1024]{1,0:T(8,128)(2,1)} %w_v.1, bf16[4096,2560]{1,0:T(8,128)(2,1)} %w_o.1, bf16[1,128]{1,0:T(2,128)(2,1)} %bitcast.4, ...), custom_call_target="tpu_custom_call" | custom-call | tf_op jit(solution)/shard_map/pallas_call | solution.py:390
  32.8 0.8 %shard_map.92 = bf16[128,2560]{1,0:T(8,128)(2,1)} custom-call(bf16[128,2560]{1,0:T(8,128)(2,1)S(1)} %shard_map.91.res_v), custom_call_target="tpu_custom_call" | custom-call | tf_op jit(solution)/shard_map/pallas_call | solution.py:426

commit v3 on v2

--- a/solution.py
+++ b/solution.py
@@ -16,6 +16,7 @@
 LANES = 128
 LOG2E = 1.4426950408889634
 AHEAD = 2
+PARTS = 1
 
 
 def rope_table(seq, head_dim):
@@ -127,31 +128,36 @@
     with jax.named_scope("barrier"):
         pl.semaphore_wait(barrier, n_dev - 1)
 
-    def far_send(h):
-        @pl.when((chip == 0) & (core == 1))
+    def on(c, k):
+        return pl.when((chip == c) & (core == k))
+
+    def far_send_wide(h):
+        @on(0, 1)
         def _():
             send(vbuf, h, 0, 3, far_sem.at[0]).start()
             send(kbuf, h, 0, 6, far_sem.at[1]).start()
             send(kbuf, h, 0, 2, far_sem.at[2]).start()
 
-        @pl.when((chip == 0) & (core == 0))
+        @on(0, 0)
         def _():
             send(vbuf, h, 0, 5, far_sem.at[0]).start()
             send(kbuf, h, 0, 4, far_sem.at[1]).start()
 
-        @pl.when((chip == 1) & (core == 0))
+        @on(1, 0)
         def _():
             send(vbuf, h, 1, 7, far_sem.at[0]).start()
             send(kbuf, h, 1, 6, far_sem.at[1]).start()
 
-        @pl.when((chip == 1) & (core == 1))
-        def _():
-            send(kbuf, h, 1, 4, far_sem.at[1]).start()
-
-        @pl.when((chip == 2) & (core == 1))
+    def far_send_near(h):
+        @on(2, 1)
         def _():
             send(vbuf, h, 2, 7, far_sem.at[0]).start()
             send(kbuf, h, 2, 6, far_sem.at[1]).start()
+
+    def far_send_transit(h):
+        @on(1, 1)
+        def _():
+            send(kbuf, h, 1, 4, far_sem.at[1]).start()
 
     def swap_in(p):
         with jax.named_scope("swap_in"):
@@ -159,10 +165,13 @@
                 swapped(kbuf, 0, 2 * p + j)
                 swapped(vbuf, 1, 2 * p + j)
 
-        @pl.when(p < AHEAD // 2)
-        def _():
-            far_send(2 * p)
-            far_send(2 * p + 1)
+        far_send_wide(2 * p)
+        far_send_wide(2 * p + 1)
+
+        @pl.when(p == 0)
+        def _():
+            for h in range(AHEAD):
+                far_send_near(h)
 
     def kv_pair(p, carry):
         with jax.named_scope("wkv_wait"):
@@ -199,8 +208,8 @@
     def q_dot(h):
         qraw[lax.rem(h, 2)] = jnp.dot(h_v[...], wq_v[lax.rem(h, wq_slots)], preferred_element_type=F32)
 
-    def q_finish(h):
-        q = qraw[lax.rem(h, 2)]
+    def q_finish(h, slot):
+        q = qraw[slot]
         for g in range(group):
             qbuf[h, g * rows:(g + 1) * rows, :] = head_norm_rotate(q[:, g * hd:(g + 1) * hd], q_gain)
 
@@ -248,95 +257,109 @@
                     @pl.when(core == 1)
                     def _():
                         arrived(kbuf, h, sc)
+        project_out(lax.rem(jnp.maximum(h - 1, 0), wo_slots))
         n_keys = 2 * (c + 1) * rows
         keys = kbuf[h, 0:2 * (c + 1)].reshape(n_keys, hd)
-        scores = lax.dot_general(keys, qbuf[h], (((1,), (1,)), ((), ())), preferred_element_type=F32)
+        vals = jnp.concatenate([vbuf[h, src] for src in range(2 * (c + 1))], axis=1)
         key_id = lax.broadcasted_iota(jnp.int32, (2 * rows, rows), 0)
         row_id = lax.broadcasted_iota(jnp.int32, (2 * rows, rows), 1)
-        visible = jnp.concatenate([key_id <= row_id + core * rows] * group, axis=1)
-        last = jnp.where(visible, scores[n_keys - 2 * rows:], -jnp.inf)
-        scores = jnp.concatenate([scores[:n_keys - 2 * rows], last], axis=0) if c else last
-        top = jnp.max(scores, axis=0, keepdims=True)
-        probs = jnp.exp2((scores - top) * score_scale)
-        total = jnp.sum(probs, axis=0, keepdims=True)
-        vals = jnp.concatenate([vbuf[h, src] for src in range(2 * (c + 1))], axis=1)
-        mixed = jnp.dot(vals, probs.astype(BF16), preferred_element_type=F32)
-        mixed_t[...] = (mixed / total).astype(BF16)
-
-    def out_dot():
+        visible = key_id <= row_id + core * rows
+        part = group * rows // PARTS
+        visible = jnp.concatenate([visible] * (group // PARTS), axis=1)
+        for i in range(PARTS):
+            cols = slice(i * part, (i + 1) * part)
+            scores = lax.dot_general(keys, qbuf[h, cols], (((1,), (1,)), ((), ())), preferred_element_type=F32)
+            last = jnp.where(visible, scores[n_keys - 2 * rows:], -jnp.inf)
+            scores = jnp.concatenate([scores[:n_keys - 2 * rows], last], axis=0) if c else last
+            top = jnp.max(scores, axis=0, keepdims=True)
+            probs = jnp.exp2((scores - top) * score_scale)
+            total = jnp.sum(probs, axis=0, keepdims=True)
+            mixed = jnp.dot(vals, probs.astype(BF16), preferred_element_type=F32)
+            mixed_t[:, cols] = (mixed / total).astype(BF16)
+
+    def project_out(slot):
         mixed = jnp.concatenate([mixed_t[:, g * rows:(g + 1) * rows].T for g in range(group)], axis=1)
-        return mixed
-
-    def project_out(h, mixed):
-        res[...] += jnp.dot(mixed, wo_v[lax.rem(h, wo_slots)], preferred_element_type=F32)
+        res[...] += jnp.dot(mixed, wo_v[slot], preferred_element_type=F32)
+
+    def relay_step(h):
+        relay(h)
+
+        @pl.when(h + AHEAD < n_kv)
+        def _():
+            far_send_near(h + AHEAD)
+        far_send_transit(h)
 
     wq_copy(2).start()
-    wo_copy(0).start()
-    swap_in(n_pairs - 1)
-    wq_wait(0)
-    q_dot(0)
-    relay(0)
     wq_copy(3).start()
-    wo_copy(1).start()
-    wq_wait(1)
-    with jax.named_scope("q_first"):
-        q_finish(0)
-        q_dot(1)
-    relay(1)
-    direct(0)
-    for r in range(0, rows, 16):
-        res[r:r + 16, :] = x_v[r:r + 16, :].astype(F32)
+
+    def q_step(h, carry):
+        wq_wait(h)
+
+        @pl.when(h < n_kv - 4)
+        def _():
+            wq_copy(h + 4).start()
+
+        @pl.when(h >= n_kv - 4)
+        def _():
+            wo_copy(h - (n_kv - 4)).start()
+
+        with jax.named_scope("q_step"):
+            q_finish(jnp.maximum(h - 1, 0), lax.rem(h + 1, 2))
+            q_dot(h)
+            some = pl.ds(pl.multiple_of(h * 16, 16), 16)
+            res[some, :] = x_v[some, :].astype(F32)
+
+        @pl.when(h == 0)
+        def _():
+            swap_in(n_pairs - 1)
+            relay_step(0)
+
+        @pl.when(lax.rem(h, 3) == 1)
+        def _():
+            relay_step(h // 3 + 1)
+
+        @pl.when(h == n_kv - 2)
+        def _():
+            direct(0)
+        return carry
+
+    lax.fori_loop(0, n_kv, q_step, 0)
+    with jax.named_scope("wo_wait"):
+        wo_copy(0).wait()
+    with jax.named_scope("q_last"):
+        q_finish(n_kv - 1, (n_kv - 1) % 2)
+    mixed_t[...] = jnp.zeros_like(mixed_t)
 
     def head_step(h, carry):
+        @pl.when(h < n_kv - 1)
+        def _():
+            direct(h + 1)
+
+        @pl.when(h > 1)
+        @jax.named_scope("wo_wait")
+        def _():
+            wo_copy(h - 1).wait()
+
         for c in range(chips):
             @pl.when(chip == c)
             @jax.named_scope("attend")
             def _():
                 attend(h, c)
 
-        @pl.when(h < n_kv - 2)
-        def _():
-            relay(h + 2)
-
-        @pl.when(h < n_kv - AHEAD)
-        def _():
-            far_send(h + AHEAD)
-
-        @pl.when(h < n_kv - 1)
-        def _():
-            direct(h + 1)
-
-        with jax.named_scope("wo_wait"):
-            wo_copy(h).wait()
-
-        @pl.when(h < n_kv - 2)
-        def _():
-            wo_copy(h + 2).start()
-            wq_wait(h + 2)
+        @pl.when((h > 0) & (h < n_kv - 3))
+        def _():
+            wo_copy(h + 3).start()
 
         @pl.when(h < n_kv - 4)
         def _():
-            wq_copy(h + 4).start()
-
-        @pl.when(h < n_kv - 2)
-        @jax.named_scope("project")
-        def _():
-            q_finish(h + 1)
-            mixed = out_dot()
-            project_out(h, mixed)
-            q_dot(h + 2)
-
-        @pl.when(h >= n_kv - 2)
-        @jax.named_scope("project_end")
-        def _():
-            @pl.when(h == n_kv - 2)
-            def _():
-                q_finish(h + 1)
-            project_out(h, out_dot())
+            relay_step(h + 4)
         return carry
 
     lax.fori_loop(0, n_kv, head_step, 0)
-    out_v[...] = res[...].astype(BF16)
+    wo_copy(n_kv - 1).wait()
+    with jax.named_scope("project"):
+        project_out((n_kv - 1) % wo_slots)
+        out_v[...] = res[...].astype(BF16)
 
     def finish(buf, sc, sem):
         part = buf.at[:, pl.ds(2 * sc, 2)]

time: 33.7 us -> 29.6 us (0.88)
  Pallas kernels: 33.6 us -> 29.5 us
    pallas_call x1, Pallas kernels: 32.7 us -> 28.7 us  [device_step(): pl.pallas_call(kernel, out_shape=pltpu.VMEM((rows, d), BF16), in_specs=[a...]
where the time goes in v3:
time: 29.6 us; the launch traced here: 29.5 us
  Pallas kernels  29.5 us (100%)
    pallas_call x1, Pallas kernels, device_step(): pl.pallas_call(kernel, out_shape=pltpu.VMEM((rows, d), BF16), in_specs=[a...  28.7 us
    pallas_call x1, Pallas kernels, device_step(): pl.pallas_call(write_back, out_shape=jax.ShapeDtypeStruct((rows, d), BF16...  0.85 us

profile of v3, /device:TPU:7, one launch (start us, length us, event | category | flops | bytes accessed | tf_op | source)
XLA Modules:
  0.0 29.5 jit_solution(7713485017302120390)
XLA Ops:
  0.0 28.7 %shard_map.91.res_v = bf16[128,2560]{1,0:T(8,128)(2,1)S(1)} custom-call(bf16[128,2560]{1,0:T(8,128)(2,1)} %x_hbm.1, bf16[20,128]{1,0:T(8,128)(2,1)} %bitcast.3, bf16[2560,4096]{1,0:T(8,128)(2,1)} %w_q.1, bf16[2560,1024]{1,0:T(8,128)(2,1)} %w_k.1, bf16[2560,1024]{1,0:T(8,128)(2,1)} %w_v.1, bf16[4096,2560]{1,0:T(8,128)(2,1)} %w_o.1, bf16[1,128]{1,0:T(2,128)(2,1)} %bitcast.4, ...), custom_call_target="tpu_custom_call" | custom-call | tf_op jit(solution)/shard_map/pallas_call | solution.py:413
  28.7 0.8 %shard_map.92 = bf16[128,2560]{1,0:T(8,128)(2,1)} custom-call(bf16[128,2560]{1,0:T(8,128)(2,1)S(1)} %shard_map.91.res_v), custom_call_target="tpu_custom_call" | custom-call | tf_op jit(solution)/shard_map/pallas_call | solution.py:449

commit v4 on v3

v4 whole, which is shorter than its diff:
```python
import functools

import jax
import jax.numpy as jnp
import numpy as np
from jax import lax
from jax.experimental import pallas as pl
from jax.experimental.pallas import tpu as pltpu
from jax.sharding import PartitionSpec as P

EPS = 1e-6
THETA = 1000000.0
MESH = pl.DeviceIdType.MESH
F32 = jnp.float32
BF16 = jnp.bfloat16
LANES = 128
LOG2E = 1.4426950408889634
AHEAD = 2
KV_FLIGHT = 8
K_BEHIND = 2


def rope_table(seq, head_dim):
    half = head_dim // 2
    inv_freq = np.power(np.float32(THETA), -(np.arange(half, dtype=np.float32) * np.float32(2.0 / head_dim))).astype(np.float32)
    angles = (np.arange(seq, dtype=np.float32)[:, None] * inv_freq[None, :]).astype(np.float32).astype(np.float64)
    return np.concatenate([np.cos(angles), np.sin(angles)], axis=1).astype(np.float32)


def kernel(x_hbm, ln_gain_hbm, w_q, w_k, w_v, w_o, q_gain_hbm, k_gain_hbm, tab_hbm, out_v,
           x_v, h_v, ln_gain, q_gain, k_gain, tab_v, wkv_v, wq_v, wo_v, kbuf, vbuf, qraw, qbuf, mixed_t, res, s_even, s_odd, top_even, top_odd,
           in_sem, wkv_sem, wq_sem, wo_sem,
           own_send, fwd_send, relay_send, k_recv, v_recv, v_relay):
    rows, d = x_v.shape
    n_kv, n_dev, _, hd = kbuf.shape
    group = qbuf.shape[1] // rows
    n_pairs = n_kv // 2
    wq_slots, wo_slots = wq_v.shape[0], wo_v.shape[0]
    chips = n_dev // 2
    me = lax.axis_index("sp")
    core = lax.rem(me, 2)
    chip = me // 2
    sibling = me + 1 - 2 * core
    score_scale = hd ** -0.5 * LOG2E

    x_copy = pltpu.make_async_copy(x_hbm, x_v, in_sem.at[0])
    small_copies = [
        pltpu.make_async_copy(ln_gain_hbm, ln_gain, in_sem.at[1]),
        pltpu.make_async_copy(q_gain_hbm, q_gain, in_sem.at[2]),
        pltpu.make_async_copy(k_gain_hbm, k_gain, in_sem.at[3]),
        pltpu.make_async_copy(tab_hbm.at[pl.ds(pl.multiple_of(me * rows, rows), rows)], tab_v, in_sem.at[4]),
    ]

    def kv_copies(h):
        cols = pl.ds(pl.multiple_of(h * hd, hd), hd)
        slot = lax.rem(h, KV_FLIGHT)
        return (pltpu.make_async_copy(w_k.at[:, cols], wkv_v.at[h, :, pl.ds(0, hd)], wkv_sem.at[slot]),
                pltpu.make_async_copy(w_v.at[:, cols], wkv_v.at[h, :, pl.ds(hd, hd)], wkv_sem.at[slot]))

    def kv_wait(h):
        pltpu.make_async_copy(wkv_v.at[h], wkv_v.at[h], wkv_sem.at[lax.rem(h, KV_FLIGHT)]).wait()

    def kv_start(h):
        for copy in kv_copies(h):
            copy.start()

    def wq_copy(h):
        n = group * hd
        slot = lax.rem(h, wq_slots)
        return pltpu.make_async_copy(w_q.at[:, pl.ds(pl.multiple_of(h * n, n), n)], wq_v.at[slot], wq_sem.at[slot])

    def wo_copy(h):
        n = group * hd
        slot = lax.rem(h, wo_slots)
        return pltpu.make_async_copy(w_o.at[pl.ds(pl.multiple_of(h * n, n), n)], wo_v.at[slot], wo_sem.at[slot])

    x_copy.start()
    for copy in small_copies:
        copy.start()
    kv_start(0)

    barrier = pltpu.get_barrier_semaphore()
    for step in range(1, n_dev):
        pl.semaphore_signal(barrier, inc=1, device_id={"sp": lax.rem(me + step, n_dev)}, device_id_type=MESH)

    def push(buf, h, blocks, dst, sem, recv=None):
        part = buf.at[h, blocks]
        recv = (k_recv if buf is kbuf else v_recv) if recv is None else recv
        return pltpu.make_async_remote_copy(src_ref=part, dst_ref=part, send_sem=sem, recv_sem=recv.at[h],
                                            device_id={"sp": dst}, device_id_type=MESH)

    def own(buf, h, dst, recv=None):
        push(buf, h, pl.ds(me, 1), dst, own_send.at[0 if buf is kbuf else 1], recv).start()

    def arrived(buf, h, n, recv=None):
        push(buf, h, pl.ds(0, n), sibling, own_send.at[0], recv).wait_recv()

    with jax.named_scope("gain_wait"):
        small_copies[0].wait()
    gain_rows = ln_gain[...].astype(F32)

    with jax.named_scope("x_wait"):
        x_copy.wait()
    for h in range(1, 4):
        kv_start(h)
    for r in range(0, rows, 16):
        xf = x_v[r:r + 16, :].astype(F32)
        norm = lax.rsqrt(jnp.mean(xf * xf, axis=-1, keepdims=True) + EPS)
        for c in range(d // LANES):
            cols = slice(c * LANES, (c + 1) * LANES)
            h_v[r:r + 16, cols] = (xf[:, cols] * norm * gain_rows[c:c + 1, :]).astype(BF16)

    kv_start(4)
    kv_start(5)
    with jax.named_scope("small_wait"):
        for copy in small_copies[1:]:
            copy.wait()
    table = tab_v[...]
    turned = pltpu.roll(table, hd // 2, 1)
    low = lax.broadcasted_iota(jnp.int32, table.shape, 1) < hd // 2
    cos_pos = jnp.where(low, table, turned)
    sin_pos = jnp.where(low, -turned, table)

    def head_norm_rotate(values, gain):
        gain = jnp.broadcast_to(gain[...].astype(F32), (8, hd))
        gain_turned = pltpu.roll(gain, hd // 2, 1)
        values = values * lax.rsqrt(jnp.mean(values * values, axis=-1, keepdims=True) + EPS)
        return (values * (cos_pos * gain[:1]) + pltpu.roll(values, hd // 2, 1) * (sin_pos * gain_turned[:1])).astype(BF16)

    with jax.named_scope("barrier"):
        pl.semaphore_wait(barrier, n_dev - 1)

    def on(c, k):
        return pl.when((chip == c) & (core == k))

    def send_wide(heads):
        @pl.when(chip == 0)
        def _():
            for h in heads:
                own(kbuf, h, 6)
                own(vbuf, h, 5, v_relay)
                own(vbuf, h, 3)
                own(kbuf, h, 2)

                @pl.when(h >= K_BEHIND)
                def _():
                    own(kbuf, h - K_BEHIND, 4)

        @pl.when(chip == 1)
        def _():
            for h in heads:
                own(kbuf, h, 6)
                own(vbuf, h, 7, v_relay)

    def send_near(h):
        @pl.when(chip == 2)
        def _():
            own(kbuf, h, 6)
            own(vbuf, h, 7)

    def send_transit(h):
        @pl.when(chip == 1)
        def _():
            own(kbuf, h, 4)

    def project_kv(heads):
        with jax.named_scope("wkv_wait"):
            for h in heads:
                kv_wait(h)
        with jax.named_scope("kv_step"):
            both = [jnp.dot(h_v[...], wkv_v[h], preferred_element_type=F32) for h in heads]
            for h, kv in zip(heads, both):
                kbuf[h, me] = head_norm_rotate(kv[:, :hd], k_gain)
                vbuf[h, me] = kv[:, hd:].T.astype(BF16)
        for h in heads:
            own(kbuf, h, sibling)
            own(vbuf, h, sibling)
        send_wide(heads)

    project_kv([0])
    send_near(0)
    kv_start(6)
    kv_start(7)
    project_kv([1])
    send_near(1)
    wq_copy(0).start()

    def kv_pair(p, carry):
        wq_copy(p).start()
        project_kv([2 * p, 2 * p + 1])
        return carry

    lax.fori_loop(1, n_pairs, kv_pair, 0)

    @pl.when(chip == 0)
    def _():
        for h in range(n_kv - K_BEHIND, n_kv):
            own(kbuf, h, 4)

    def q_dot(h):
        qraw[lax.rem(h, 2)] = jnp.dot(h_v[...], wq_v[lax.rem(h, wq_slots)], preferred_element_type=F32)

    def q_finish(h, slot):
        q = qraw[slot]
        for g in range(group):
            qbuf[h, g * rows:(g + 1) * rows, :] = head_norm_rotate(q[:, g * hd:(g + 1) * hd], q_gain)

    def wq_wait(h):
        with jax.named_scope("wq_wait"):
            wq_copy(h).wait()

    def relay(h, c):
        @pl.when((chip == c) & (core == 1))
        @jax.named_scope("relay")
        def _():
            blocks = pl.ds(2 * (c - 2), 2)
            arrived(vbuf, h, 2, v_relay)
            push(vbuf, h, blocks, sibling, fwd_send).start()
            push(vbuf, h, blocks, 11 - 2 * c, relay_send).start()

    def direct_k(h):
        for c in range(chips):
            @pl.when((chip == c) & (core == 0))
            @jax.named_scope("direct_k")
            def _():
                arrived(kbuf, h, 2 * c + 1)
                if c:
                    push(kbuf, h, pl.ds(0, 2 * c), sibling, fwd_send).start()

    def direct_v(h):
        for c in range(chips):
            @pl.when((chip == c) & (core == 1))
            @jax.named_scope("direct_v")
            def _():
                if c < 2:
                    arrived(vbuf, h, 2 * c + 1)
                    if c:
                        push(vbuf, h, pl.ds(0, 2), sibling, fwd_send).start()
                elif c == 2:
                    arrived(vbuf, h, 3)
                    push(vbuf, h, pl.ds(2, 2), sibling, fwd_send).start()
                else:
                    arrived(vbuf, h, 5)
                    push(vbuf, h, pl.ds(0, 2), sibling, fwd_send).start()
                    push(vbuf, h, pl.ds(4, 2), sibling, fwd_send).start()

    def wait_k(h, c):
        @pl.when(core == 1)
        @jax.named_scope("wait_k")
        def _():
            arrived(kbuf, h, 2 * c + 1)

    def wait_v(h, c):
        @pl.when(core == 0)
        @jax.named_scope("wait_v")
        def _():
            arrived(vbuf, h, 2 * c + 1)

    def make_scores(h, c, s_out, top_out):
        n_keys = 2 * (c + 1) * rows
        keys = kbuf[h, 0:2 * (c + 1)].reshape(n_keys, hd)
        key_id = lax.broadcasted_iota(jnp.int32, (2 * rows, rows), 0)
        row_id = lax.broadcasted_iota(jnp.int32, (2 * rows, rows), 1)
        visible = jnp.concatenate([key_id <= row_id + core * rows] * group, axis=1)
        scores = lax.dot_general(keys, qbuf[h], (((1,), (1,)), ((), ())), preferred_element_type=F32)
        last = jnp.where(visible, scores[n_keys - 2 * rows:], -jnp.inf)
        scores = jnp.concatenate([scores[:n_keys - 2 * rows], last], axis=0) if c else last
        s_out[0:n_keys, :] = scores
        top_out[...] = jnp.broadcast_to(jnp.max(scores, axis=0, keepdims=True), top_out.shape)

    def mix(h, c, s_in, top_in):
        n_keys = 2 * (c + 1) * rows
        vals = jnp.concatenate([vbuf[h, src] for src in range(2 * (c + 1))], axis=1)
        probs = jnp.exp2((s_in[0:n_keys, :] - top_in[0:1, :]) * score_scale)
        total = jnp.sum(probs, axis=0, keepdims=True)
        mixed = jnp.dot(vals, probs.astype(BF16), preferred_element_type=F32)
        mixed_t[...] = (mixed / total).astype(BF16)

    def project_out(slot):
        mixed = jnp.concatenate([mixed_t[:, g * rows:(g + 1) * rows].T for g in range(group)], axis=1)
        res[...] += jnp.dot(mixed, wo_v[slot], preferred_element_type=F32)

    def relay_step(h):
        relay(h, 2)

        @pl.when(h + AHEAD < n_kv)
        def _():
            send_near(h + AHEAD)
        send_transit(h)

    def q_step(h, carry):
        wq_wait(h)

        @pl.when(h < n_kv - 4)
        def _():
            wq_copy(h + 4).start()

        @pl.when(h >= n_kv - 4)
        def _():
            wo_copy(h - (n_kv - 4)).start()

        with jax.named_scope("q_step"):
            q_finish(jnp.maximum(h - 1, 0), lax.rem(h + 1, 2))
            q_dot(h)
            some = pl.ds(pl.multiple_of(h * 16, 16), 16)
            res[some, :] = x_v[some, :].astype(F32)

        @pl.when(h == 0)
        def _():
            relay_step(0)

        @pl.when(lax.rem(h, 3) == 1)
        def _():
            relay_step(h // 3 + 1)

        @pl.when((h == n_kv - 5) | (h == n_kv - 3))
        def _():
            relay(h // 2 - 1, 3)
            direct_k(h // 2 - 1)

        @pl.when(h == n_kv - 2)
        def _():
            direct_v(0)
        return carry

    lax.fori_loop(0, n_kv, q_step, 0)
    with jax.named_scope("wo_wait"):
        wo_copy(0).wait()
    mixed_t[...] = jnp.zeros_like(mixed_t)

    for c in range(chips):
        @pl.when(chip == c)
        def _():
            wait_k(0, c)
            with jax.named_scope("first_scores"):
                make_scores(0, c, s_even, top_even)
                q_finish(n_kv - 1, (n_kv - 1) % 2)

    def head_step(h, this, other, tail):
        @pl.when(h < n_kv - 2)
        def _():
            direct_k(h + 2)
            relay(h + 2, 3)
            direct_v(h + 1)

        @pl.when(h > 1)
        @jax.named_scope("wo_wait")
        def _():
            wo_copy(h - 1).wait()

        for c in range(chips):
            @pl.when(chip == c)
            def _():
                def block(more):
                    wait_v(h, c)
                    if more:
                        wait_k(h + 1, c)
                    with jax.named_scope("attend"):
                        if more:
                            project_out(lax.rem(jnp.maximum(h - 1, 0), wo_slots))
                            make_scores(h + 1, c, *other)
                        mix(h, c, *this)

                if not tail:
                    block(True)
                else:
                    @pl.when(h < n_kv - 1)
                    def _():
                        block(True)

                    @pl.when(h == n_kv - 1)
                    def _():
                        with jax.named_scope("project"):
                            project_out((n_kv - 2) % wo_slots)
                        block(False)

        if not tail:
            @pl.when(h == n_kv - 2)
            def _():
                direct_v(n_kv - 1)

        @pl.when((h > 0) & (h < n_kv - 3))
        def _():
            wo_copy(h + 3).start()

        @pl.when(h < n_kv - 4)
        def _():
            relay_step(h + 4)

    def two_heads(i, carry):
        head_step(2 * i, (s_even, top_even), (s_odd, top_odd), False)
        head_step(2 * i + 1, (s_odd, top_odd), (s_even, top_even), True)
        return carry

    lax.fori_loop(0, n_kv // 2, two_heads, 0)
    wo_copy(n_kv - 1).wait()
    with jax.named_scope("project"):
        project_out((n_kv - 1) % wo_slots)
        out_v[...] = res[...].astype(BF16)

    def sent(buf, heads, blocks, sem):
        part = buf.at[0:heads, 0:blocks]
        pltpu.make_async_remote_copy(src_ref=part, dst_ref=part, send_sem=sem, recv_sem=k_recv.at[0],
                                     device_id={"sp": sibling}, device_id_type=MESH).wait_send()

    with jax.named_scope("finish_sends"):
        for c in range(chips):
            @pl.when(chip == c)
            def _():
                sent(kbuf, n_kv, (4, 3, 2, 1)[c], own_send.at[0])
                sent(vbuf, n_kv, (3, 2, 2, 1)[c], own_send.at[1])
                if c:
                    sent(kbuf, n_kv, 2 * c, fwd_send)
                if c >= 2:
                    @pl.when(core == 1)
                    def _():
                        sent(vbuf, n_kv, 2, relay_send)


def write_back(res_v, out_hbm, sem):
    copy = pltpu.make_async_copy(res_v, out_hbm, sem)
    copy.start()
    copy.wait()


def solution(mesh):
    def device_step(hidden, ln_gain, w_q, w_k, w_v, w_o, q_gain, k_gain):
        rows, d = hidden.shape
        hd = q_gain.shape[0]
        n_kv = w_k.shape[1] // hd
        group = w_q.shape[1] // w_k.shape[1]
        n_dev = mesh.shape['sp']
        table = jnp.asarray(rope_table(rows * n_dev, hd))
        any_spec = pl.BlockSpec(memory_space=pl.ANY)
        vmem_spec = pl.BlockSpec(memory_space=pltpu.VMEM)
        dma = pltpu.SemaphoreType.DMA
        result = pl.pallas_call(
            kernel,
            out_shape=pltpu.VMEM((rows, d), BF16),
            in_specs=[any_spec] * 9,
            out_specs=vmem_spec,
            scratch_shapes=[
                pltpu.VMEM((rows, d), BF16),
                pltpu.VMEM((rows, d), BF16),
                pltpu.VMEM((d // LANES, LANES), BF16),
                pltpu.VMEM((1, hd), BF16),
                pltpu.VMEM((1, hd), BF16),
                pltpu.VMEM((rows, hd), F32),
                pltpu.VMEM((n_kv, d, 2 * hd), BF16),
                pltpu.VMEM((5, d, group * hd), BF16),
                pltpu.VMEM((4, group * hd, d), BF16),
                pltpu.VMEM((n_kv, n_dev, rows, hd), BF16),
                pltpu.VMEM((n_kv, n_dev, hd, rows), BF16),
                pltpu.VMEM((2, rows, group * hd), F32),
                pltpu.VMEM((n_kv, group * rows, hd), BF16),
                pltpu.VMEM((hd, group * rows), BF16),
                pltpu.VMEM((rows, d), F32),
                pltpu.VMEM((rows * n_dev, group * rows), F32),
                pltpu.VMEM((rows * n_dev, group * rows), F32),
                pltpu.VMEM((8, group * rows), F32),
                pltpu.VMEM((8, group * rows), F32),
                dma((5,)),
                dma((KV_FLIGHT,)),
                dma((5,)),
                dma((4,)),
                dma((2,)),
                dma,
                dma,
                dma((n_kv,)),
                dma((n_kv,)),
                dma((n_kv,)),
            ],
            compiler_params=pltpu.CompilerParams(collective_id=0, has_side_effects=True, vmem_limit_bytes=62000000),
        )(hidden, ln_gain.reshape(-1, LANES), w_q, w_k, w_v, w_o, q_gain.reshape(1, -1), k_gain.reshape(1, -1), table)
        return pl.pallas_call(
            write_back,
            out_shape=jax.ShapeDtypeStruct((rows, d), BF16),
            in_specs=[vmem_spec],
            out_specs=any_spec,
            scratch_shapes=[dma],
            compiler_params=pltpu.CompilerParams(vmem_limit_bytes=1000000),
        )(result)

    row_spec = P(('dp', 'sp'), None)
    return jax.shard_map(device_step, mesh=mesh, in_specs=(row_spec, P(), P(), P(), P(), P(), P(), P()), out_specs=row_spec, check_vma=False)
```

time: 29.6 us -> 27.7 us (0.936)
  the two profiles are of different devices: /device:TPU:7 before, /device:TPU:5 now
where the time goes in v4:
time: 27.7 us; the launch traced here: 27.6 us
  Pallas kernels  27.4 us (99%)
    pallas_call x1, Pallas kernels, device_step(): pl.pallas_call(kernel, out_shape=pltpu.VMEM((rows, d), BF16), in_specs=[a...  26.6 us
    pallas_call x1, Pallas kernels, device_step(): pl.pallas_call(write_back, out_shape=jax.ShapeDtypeStruct((rows, d), BF16...  0.85 us

profile of v4, /device:TPU:5, one launch (start us, length us, event | category | flops | bytes accessed | tf_op | source)
XLA Modules:
  0.0 27.6 jit_solution(17028728433826667529)
XLA Ops:
  0.0 26.6 %shard_map.91.res_v = bf16[128,2560]{1,0:T(8,128)(2,1)S(1)} custom-call(bf16[128,2560]{1,0:T(8,128)(2,1)} %x_hbm.1, bf16[20,128]{1,0:T(8,128)(2,1)} %bitcast.3, bf16[2560,4096]{1,0:T(8,128)(2,1)} %w_q.1, bf16[2560,1024]{1,0:T(8,128)(2,1)} %w_k.1, bf16[2560,1024]{1,0:T(8,128)(2,1)} %w_v.1, bf16[4096,2560]{1,0:T(8,128)(2,1)} %w_o.1, bf16[1,128]{1,0:T(2,128)(2,1)} %bitcast.4, ...), custom_call_target="tpu_custom_call" | custom-call | tf_op jit(solution)/shard_map/pallas_call | solution.py:437
  26.6 0.8 %shard_map.92 = bf16[128,2560]{1,0:T(8,128)(2,1)} custom-call(bf16[128,2560]{1,0:T(8,128)(2,1)S(1)} %shard_map.91.res_v), custom_call_target="tpu_custom_call" | custom-call | tf_op jit(solution)/shard_map/pallas_call | solution.py:475

commit v5 on v4

--- a/solution.py
+++ b/solution.py
@@ -149,8 +149,8 @@
         @pl.when(chip == 1)
         def _():
             for h in heads:
+                own(vbuf, h, 7, v_relay)
                 own(kbuf, h, 6)
-                own(vbuf, h, 7, v_relay)
 
     def send_near(h):
         @pl.when(chip == 2)
@@ -217,6 +217,8 @@
             arrived(vbuf, h, 2, v_relay)
             push(vbuf, h, blocks, sibling, fwd_send).start()
             push(vbuf, h, blocks, 11 - 2 * c, relay_send).start()
+            if c == 3:
+                push(vbuf, h, blocks, 4, relay_send).start()
 
     def direct_k(h):
         for c in range(chips):
@@ -227,8 +229,8 @@
                 if c:
                     push(kbuf, h, pl.ds(0, 2 * c), sibling, fwd_send).start()
 
-    def direct_v(h):
-        for c in range(chips):
+    def direct_v(h, those=range(4)):
+        for c in those:
             @pl.when((chip == c) & (core == 1))
             @jax.named_scope("direct_v")
             def _():
@@ -236,10 +238,7 @@
                     arrived(vbuf, h, 2 * c + 1)
                     if c:
                         push(vbuf, h, pl.ds(0, 2), sibling, fwd_send).start()
-                elif c == 2:
-                    arrived(vbuf, h, 3)
-                    push(vbuf, h, pl.ds(2, 2), sibling, fwd_send).start()
-                else:
+                elif c == 3:
                     arrived(vbuf, h, 5)
                     push(vbuf, h, pl.ds(0, 2), sibling, fwd_send).start()
                     push(vbuf, h, pl.ds(4, 2), sibling, fwd_send).start()
@@ -255,6 +254,12 @@
         @jax.named_scope("wait_v")
         def _():
             arrived(vbuf, h, 2 * c + 1)
+
+        if c == 2:
+            @pl.when(core == 1)
+            @jax.named_scope("wait_v")
+            def _():
+                arrived(vbuf, h, 3)
 
     def make_scores(h, c, s_out, top_out):
         n_keys = 2 * (c + 1) * rows
@@ -313,9 +318,12 @@
         def _():
             relay_step(h // 3 + 1)
 
+        @pl.when((h == n_kv - 5) | (h == n_kv - 3) | (h == n_kv - 1))
+        def _():
+            relay(h // 2 - 1, 3)
+
         @pl.when((h == n_kv - 5) | (h == n_kv - 3))
         def _():
-            relay(h // 2 - 1, 3)
             direct_k(h // 2 - 1)
 
         @pl.when(h == n_kv - 2)
@@ -340,8 +348,18 @@
         @pl.when(h < n_kv - 2)
         def _():
             direct_k(h + 2)
+
+        @pl.when((h > 0) & (h < n_kv - 2))
+        def _():
             relay(h + 2, 3)
-            direct_v(h + 1)
+
+        @pl.when(h < n_kv - 2)
+        def _():
+            direct_v(h + 1, range(chips - 1))
+
+        @pl.when(h < n_kv - 1)
+        def _():
+            direct_v(h + 1, [chips - 1])
 
         @pl.when(h > 1)
         @jax.named_scope("wo_wait")
@@ -370,14 +388,20 @@
 
                     @pl.when(h == n_kv - 1)
                     def _():
-                        with jax.named_scope("project"):
-                            project_out((n_kv - 2) % wo_slots)
-                        block(False)
+                        if c >= chips - 2:
+                            wait_v(h, c)
+                            with jax.named_scope("attend"):
+                                project_out((n_kv - 2) % wo_slots)
+                                mix(h, c, *this)
+                        else:
+                            with jax.named_scope("project"):
+                                project_out((n_kv - 2) % wo_slots)
+                            block(False)
 
         if not tail:
             @pl.when(h == n_kv - 2)
             def _():
-                direct_v(n_kv - 1)
+                direct_v(n_kv - 1, range(chips - 1))
 
         @pl.when((h > 0) & (h < n_kv - 3))
         def _():
@@ -409,12 +433,21 @@
             def _():
                 sent(kbuf, n_kv, (4, 3, 2, 1)[c], own_send.at[0])
                 sent(vbuf, n_kv, (3, 2, 2, 1)[c], own_send.at[1])
-                if c:
+                if c in (1, 3):
                     sent(kbuf, n_kv, 2 * c, fwd_send)
-                if c >= 2:
+                if c == 2:
+                    @pl.when(core == 0)
+                    def _():
+                        sent(kbuf, n_kv, 4, fwd_send)
+
                     @pl.when(core == 1)
                     def _():
+                        sent(vbuf, n_kv, 2, fwd_send)
                         sent(vbuf, n_kv, 2, relay_send)
+                if c == 3:
+                    @pl.when(core == 1)
+                    def _():
+                        sent(vbuf, n_kv, 4, relay_send)
 
 
 def write_back(res_v, out_hbm, sem):

time: 27.7 us -> 27.5 us (level)
  the two profiles are of different devices: /device:TPU:5 before, /device:TPU:4 now
where the time goes in v5:
time: 27.5 us; the launch traced here: 27.4 us
  Pallas kernels  27.3 us (99%)
    pallas_call x1, Pallas kernels, device_step(): pl.pallas_call(kernel, out_shape=pltpu.VMEM((rows, d), BF16), in_specs=[a...  26.4 us
    pallas_call x1, Pallas kernels, device_step(): pl.pallas_call(write_back, out_shape=jax.ShapeDtypeStruct((rows, d), BF16...  0.85 us

profile of v5, /device:TPU:4, one launch (start us, length us, event | category | flops | bytes accessed | tf_op | source)
XLA Modules:
  0.0 27.4 jit_solution(11806415345523780508)
XLA Ops:
  0.0 26.4 %shard_map.91.res_v = bf16[128,2560]{1,0:T(8,128)(2,1)S(1)} custom-call(bf16[128,2560]{1,0:T(8,128)(2,1)} %x_hbm.1, bf16[20,128]{1,0:T(8,128)(2,1)} %bitcast.3, bf16[2560,4096]{1,0:T(8,128)(2,1)} %w_q.1, bf16[2560,1024]{1,0:T(8,128)(2,1)} %w_k.1, bf16[2560,1024]{1,0:T(8,128)(2,1)} %w_v.1, bf16[4096,2560]{1,0:T(8,128)(2,1)} %w_o.1, bf16[1,128]{1,0:T(2,128)(2,1)} %bitcast.4, ...), custom_call_target="tpu_custom_call" | custom-call | tf_op jit(solution)/shard_map/pallas_call | solution.py:470
  26.4 0.8 %shard_map.92 = bf16[128,2560]{1,0:T(8,128)(2,1)} custom-call(bf16[128,2560]{1,0:T(8,128)(2,1)S(1)} %shard_map.91.res_v), custom_call_target="tpu_custom_call" | custom-call | tf_op jit(solution)/shard_map/pallas_call | solution.py:508

commit v6 on v5

--- a/solution.py
+++ b/solution.py
@@ -74,8 +74,10 @@
         slot = lax.rem(h, wo_slots)
         return pltpu.make_async_copy(w_o.at[pl.ds(pl.multiple_of(h * n, n), n)], wo_v.at[slot], wo_sem.at[slot])
 
+    small_copies[0].start()
     x_copy.start()
-    for copy in small_copies:
+    small_copies[3].start()
+    for copy in small_copies[1:3]:
         copy.start()
     kv_start(0)
 

time: 27.5 us -> 27.6 us (level)
  no operation moved by 1% of the time
where the time goes in v6:
time: 27.6 us; the launch traced here: 27.5 us
  Pallas kernels  27.3 us (99%)
    pallas_call x1, Pallas kernels, device_step(): pl.pallas_call(kernel, out_shape=pltpu.VMEM((rows, d), BF16), in_specs=[a...  26.4 us
    pallas_call x1, Pallas kernels, device_step(): pl.pallas_call(write_back, out_shape=jax.ShapeDtypeStruct((rows, d), BF16...  0.85 us

profile of v6, /device:TPU:4, one launch (start us, length us, event | category | flops | bytes accessed | tf_op | source)
XLA Modules:
  0.0 27.5 jit_solution(609976289109394934)
XLA Ops:
  0.0 26.4 %shard_map.91.res_v = bf16[128,2560]{1,0:T(8,128)(2,1)S(1)} custom-call(bf16[128,2560]{1,0:T(8,128)(2,1)} %x_hbm.1, bf16[20,128]{1,0:T(8,128)(2,1)} %bitcast.3, bf16[2560,4096]{1,0:T(8,128)(2,1)} %w_q.1, bf16[2560,1024]{1,0:T(8,128)(2,1)} %w_k.1, bf16[2560,1024]{1,0:T(8,128)(2,1)} %w_v.1, bf16[4096,2560]{1,0:T(8,128)(2,1)} %w_o.1, bf16[1,128]{1,0:T(2,128)(2,1)} %bitcast.4, ...), custom_call_target="tpu_custom_call" | custom-call | tf_op jit(solution)/shard_map/pallas_call | solution.py:472
  26.5 0.8 %shard_map.92 = bf16[128,2560]{1,0:T(8,128)(2,1)} custom-call(bf16[128,2560]{1,0:T(8,128)(2,1)S(1)} %shard_map.91.res_v), custom_call_target="tpu_custom_call" | custom-call | tf_op jit(solution)/shard_map/pallas_call | solution.py:510
